TPU v7x, 512 devices: a 8x2x16 block of a 8x8x16 slice. The times are simulated.
512 devices in a mesh: grp: 2 (over y), ha: 16 (over z), ta: 8 (over x), cam: 2 (over core).
Axes of the slice: x: 8, y: 2, z: 16, core: 2. Of those that a mesh axis runs over, the one named last changes fastest.
The devices are a block of a 8x8x16 slice.
Arguments:
- video: bfloat16 [4, 32, 128, 48, 128], P(('grp', 'cam'), 'ta', 'ha'), parts along dimension 0, may hold values from -6 to 6
- norm1_gain: float32 [128], replicated, may hold values from 0.1 to 1.9
- norm1_shift: float32 [128], replicated, may hold values from -3 to 3
- conv1_weight: bfloat16 [3, 3, 3, 128, 128], replicated, may hold values from -0.109375 to 0.109375
- conv1_bias: float32 [128], replicated, may hold values from -3 to 3
- norm2_gain: float32 [128], replicated, may hold values from 0.1 to 1.9
- norm2_shift: float32 [128], replicated, may hold values from -3 to 3
- conv2_weight: bfloat16 [3, 3, 3, 128, 128], replicated, may hold values from -0.109375 to 0.109375
- conv2_bias: float32 [128], replicated, may hold values from -3 to 3
Outputs:
- encoded: bfloat16 [4, 32, 128, 48, 128], P(('grp', 'cam'), 'ta', 'ha'), parts along dimension 0
There are 2 independent parts, one for each index of `grp`. A program takes and returns all parts, laid end to end along the dimension named above; an argument that names none is the same for every part. Nothing has to cross between parts.
All inputs are finite; a program needn't handle non-finite values.
Results may differ from a plain program's by a relative error of at most 0.0039.
Values may be sent and summed in bfloat16 or wider, within the bound.
No kernel may reach another device: no remote copies, remote signals or barrier semaphores. Data moves between devices by JAX's collectives and lax.ppermute only.
A program may use at most 128 MiB of HBM per device.

v0:
```python
import jax
import jax.numpy as jnp
from jax import lax
from jax.sharding import PartitionSpec as P


def from_behind(shard, axis, by):
    length = lax.axis_size(axis)
    pairs = [(i, i + by) for i in range(length) if 0 <= i + by < length]
    return lax.ppermute(shard, axis, pairs)


def padded_2(cells, sides, width):
    for axis, dim in sides:
        count = lax.axis_size(axis)
        ends = count - 1
        head = lax.slice_in_dim(cells, 0, width, axis=dim)
        tail = lax.slice_in_dim(cells, cells.shape[dim] - width, cells.shape[dim], axis=dim)
        cells = jnp.concatenate(
            [
                lax.ppermute(tail, axis, [(i, (i + 1) % count) for i in range(ends)]),
                cells,
                lax.ppermute(head, axis, [((i + 1) % count, i) for i in range(ends)]),
            ],
            axis=dim,
        )
    return cells


def activate(values, gain, shift):
    middle = jnp.mean(values, axis=-1, keepdims=True)
    centred = values - middle
    spread = jnp.mean(centred * centred, axis=-1, keepdims=True)
    normed = centred * lax.rsqrt(spread + 1e-06) * gain + shift
    return jax.nn.silu(normed)


def widen(padded):
    return jnp.pad(padded, ((0, 0), (0, 0), (1, 1), (0, 0)))


def conv_valid(padded, weight):
    out_frames = padded.shape[0] - 2
    out_rows = padded.shape[1] - 2
    out_cols = padded.shape[2] - 2
    channels = weight.shape[4]
    summed = jnp.zeros((out_frames, out_rows, out_cols, channels), jnp.float32)
    for step_t in range(3):
        for step_h in range(3):
            for step_w in range(3):
                window = padded[
                    step_t : step_t + out_frames,
                    step_h : step_h + out_rows,
                    step_w : step_w + out_cols,
                ]
                summed = summed + jnp.einsum(
                    "fhwc,cd->fhwd",
                    window,
                    weight[step_t, step_h, step_w],
                    preferred_element_type=jnp.float32,
                )
    return summed


def causal_layer(layer_input, weight, span_index):
    earlier = from_behind(layer_input[-2:], "ta", 1)
    leading = jnp.broadcast_to(layer_input[:1], earlier.shape)
    earlier = jnp.where(span_index == 0, leading, earlier)
    extended = jnp.concatenate([earlier, layer_input], axis=0)
    extended = padded_2(extended, (("ha", 1),), 1)
    return conv_valid(widen(extended), weight)


def body(
    video,
    norm1_gain,
    norm1_shift,
    conv1_weight,
    conv1_bias,
    norm2_gain,
    norm2_shift,
    conv2_weight,
    conv2_bias,
):
    camera_clip = video[0]
    span_index = lax.axis_index("ta")
    inputs = camera_clip.astype(jnp.float32)
    first_input = activate(inputs, norm1_gain, norm1_shift).astype(jnp.bfloat16)
    first_out = causal_layer(first_input, conv1_weight, span_index) + conv1_bias
    second_input = activate(first_out, norm2_gain, norm2_shift).astype(jnp.bfloat16)
    second_out = causal_layer(second_input, conv2_weight, span_index) + conv2_bias
    encoded = (inputs + second_out).astype(jnp.bfloat16)
    return encoded[None]


def solution(mesh):
    placed = (P(("grp", "cam"), "ta", "ha", None, None), P(), P(), P(), P(), P(), P(), P(), P())
    return jax.shard_map(
        body,
        mesh=mesh,
        in_specs=placed,
        out_specs=P(("grp", "cam"), "ta", "ha", None, None),
        check_vma=False,
    )
```

profile of v0, /device:TPU:66, one launch (start us, length us, event | category | flops | bytes accessed | tf_op | source)
XLA Modules:
  0.0 89.4 jit_solution(7438171737041188819)
XLA Ops:
  0.0 1.3 %convert_reduce_fusion = f32[4,8,48]{2,1,0:T(8,128)S(1)} fusion(bf16[1,4,8,48,128]{4,3,2,1,0:T(8,128)(2,1)} %param.9), kind=kLoop, calls=%fused_computation.61 | loop fusion | flops 391680 | bytes 399360 | tf_op jit(solution)/shard_map/reduce_sum | solution.py:31
  1.4 1.5 %fusion.51 = f32[4,8,48]{2,1,0:T(8,128)S(1)} fusion(bf16[1,4,8,48,128]{4,3,2,1,0:T(8,128)(2,1)} %param.9, f32[4,8,48]{2,1,0:T(8,128)S(1)} %broadcast_multiply_fusion.1), kind=kLoop, calls=%fused_computation.78 | loop fusion | flops 784896 | bytes 405504 | tf_op jit(solution)/shard_map/reduce_sum | solution.py:33
  2.9 0.5 fusion.59
  3.5 3.7 %collective-permute-start = (bf16[2,8,48,128]{3,2,1,0:T(8,128)(2,1)S(1)}, bf16[2,8,48,128]{3,2,1,0:T(8,128)(2,1)S(1)}, u32[]{:S(2)}, u32[]{:S(2)}) collective-permute-start(bf16[2,8,48,128]{3,2,1,0:T(8,128)(2,1)S(1)} %slice.495), channel_id=1, source_target_pairs={{0,2},{2,4},{4,6},{6,8},{8,10},{10,12},{12,14},{1,3},{3,5},{5,7},{... | collective-permute-start | bytes 589832 | tf_op jit(solution)/shard_map/ppermute | solution.py:10
  7.2 41.7 %collective-permute-done = bf16[2,8,48,128]{3,2,1,0:T(8,128)(2,1)S(1)} collective-permute-done((bf16[2,8,48,128]{3,2,1,0:T(8,128)(2,1)S(1)}, bf16[2,8,48,128]{3,2,1,0:T(8,128)(2,1)S(1)}, u32[]{:S(2)}, u32[]{:S(2)}) %collective-permute-start) | collective-permute-done | bytes 196640 | tf_op jit(solution)/shard_map/ppermute | solution.py:10
  49.0 1.3 %collective-permute-start.1 = (bf16[6,1,48,128]{3,2,1,0:T(8,128)(2,1)S(1)}, bf16[6,1,48,128]{3,2,1,0:T(8,128)(2,1)S(1)}, u32[]{:S(2)}, u32[]{:S(2)}) collective-permute-start(bf16[6,1,48,128]{3,2,1,0:T(8,128)(2,1)S(1)} %get-tuple-element.7), channel_id=1, source_target_pairs={{0,16},{16,32},{32,48},{48,64},{64,80},{80,96},{96,112},{112,128},... | collective-permute-start | bytes 221192 | tf_op jit(solution)/shard_map/ppermute | solution.py:21
  50.3 1.3 %collective-permute-start.2 = (bf16[6,1,48,128]{3,2,1,0:T(8,128)(2,1)S(1)}, bf16[6,1,48,128]{3,2,1,0:T(8,128)(2,1)S(1)}, u32[]{:S(2)}, u32[]{:S(2)}) collective-permute-start(bf16[6,1,48,128]{3,2,1,0:T(8,128)(2,1)S(1)} %get-tuple-element.8), channel_id=1, source_target_pairs={{16,0},{32,16},{48,32},{64,48},{80,64},{96,80},{112,96},{128,112},... | collective-permute-start | bytes 221192 | tf_op jit(solution)/shard_map/ppermute | solution.py:23
  51.6 0.6 fusion.70
  52.2 4.3 %collective-permute-done.2 = bf16[6,1,48,128]{3,2,1,0:T(8,128)(2,1)S(1)} collective-permute-done((bf16[6,1,48,128]{3,2,1,0:T(8,128)(2,1)S(1)}, bf16[6,1,48,128]{3,2,1,0:T(8,128)(2,1)S(1)}, u32[]{:S(2)}, u32[]{:S(2)}) %collective-permute-start.2) | collective-permute-done | bytes 73760 | tf_op jit(solution)/shard_map/ppermute | solution.py:23
  56.6 0.4 fusion.48
  62.0 0.3 fusion.33
  62.3 0.3 fusion.31
  62.6 0.3 fusion.29
  62.9 0.3 fusion.27
  63.2 0.4 fusion.25
  63.6 0.3 copy-done.5
  63.8 0.4 fusion.259
  64.3 0.5 multiply_reduce_fusion
  65.0 0.5 multiply_convert_fusion
  65.5 2.1 %collective-permute-start.3 = (bf16[2,8,48,128]{3,2,1,0:T(8,128)(2,1)S(1)}, bf16[2,8,48,128]{3,2,1,0:T(8,128)(2,1)S(1)}, u32[]{:S(2)}, u32[]{:S(2)}) collective-permute-start(bf16[2,8,48,128]{3,2,1,0:T(8,128)(2,1)S(1)} %slice.515), channel_id=1, source_target_pairs={{0,2},{2,4},{4,6},{6,8},{8,10},{10,12},{12,14},{1,3},{3,5},{5,7},{... | collective-permute-start | bytes 589832 | tf_op jit(solution)/shard_map/ppermute | solution.py:10
  67.6 5.6 %collective-permute-done.3 = bf16[2,8,48,128]{3,2,1,0:T(8,128)(2,1)S(1)} collective-permute-done((bf16[2,8,48,128]{3,2,1,0:T(8,128)(2,1)S(1)}, bf16[2,8,48,128]{3,2,1,0:T(8,128)(2,1)S(1)}, u32[]{:S(2)}, u32[]{:S(2)}) %collective-permute-start.3) | collective-permute-done | bytes 196640 | tf_op jit(solution)/shard_map/ppermute | solution.py:10
  73.3 1.6 %collective-permute-start.4 = (bf16[6,1,48,128]{3,2,1,0:T(8,128)(2,1)S(1)}, bf16[6,1,48,128]{3,2,1,0:T(8,128)(2,1)S(1)}, u32[]{:S(2)}, u32[]{:S(2)}) collective-permute-start(bf16[6,1,48,128]{3,2,1,0:T(8,128)(2,1)S(1)} %get-tuple-element.5), channel_id=1, source_target_pairs={{0,16},{16,32},{32,48},{48,64},{64,80},{80,96},{96,112},{112,128},... | collective-permute-start | bytes 221192 | tf_op jit(solution)/shard_map/ppermute | solution.py:21
  74.9 1.5 %collective-permute-start.5 = (bf16[6,1,48,128]{3,2,1,0:T(8,128)(2,1)S(1)}, bf16[6,1,48,128]{3,2,1,0:T(8,128)(2,1)S(1)}, u32[]{:S(2)}, u32[]{:S(2)}) collective-permute-start(bf16[6,1,48,128]{3,2,1,0:T(8,128)(2,1)S(1)} %get-tuple-element.6), channel_id=1, source_target_pairs={{16,0},{32,16},{48,32},{64,48},{80,64},{96,80},{112,96},{128,112},... | collective-permute-start | bytes 221192 | tf_op jit(solution)/shard_map/ppermute | solution.py:23
  76.8 4.3 %collective-permute-done.5 = bf16[6,1,48,128]{3,2,1,0:T(8,128)(2,1)S(1)} collective-permute-done((bf16[6,1,48,128]{3,2,1,0:T(8,128)(2,1)S(1)}, bf16[6,1,48,128]{3,2,1,0:T(8,128)(2,1)S(1)}, u32[]{:S(2)}, u32[]{:S(2)}) %collective-permute-start.5) | collective-permute-done | bytes 73760 | tf_op jit(solution)/shard_map/ppermute | solution.py:23
  81.1 0.4 select_maximum_fusion
  83.3 0.3 fusion.88
  84.3 0.3 fusion.76
  86.6 0.3 fusion.16
  86.9 0.3 fusion.14
  87.7 0.4 fusion.8
  88.1 0.3 copy-done.8
  88.4 1.1 %fusion.37 = bf16[1,4,8,48,128]{4,3,2,1,0:T(8,128)(2,1)} fusion(f32[4,8,48,128]{3,2,1,0:T(8,128)S(1)} %fusion.72, f32[4,8,48,128]{3,2,1,0:T(8,128)S(1)} %fusion.8, bf16[1,4,8,48,128]{4,3,2,1,0:T(8,128)(2,1)S(1)} %copy-done, f32[128]{0:T(128)S(1)} %copy-done.8, bf16[3,3,3,128,128]{4,3,2,1,0:T(8,128)(2,1)S(1)} %copy-done.1, ...), kind=kOutput, calls=%fused_computation.59 | convolution fusion | flops 53501952 | bytes 3056128 | tf_op jit(solution)/shard_map/fhwc,cd->fhwd/dot_general | solution.py:56
  (71 shorter events, 10.8 us)
Async XLA Ops:
  0.0 2.9 %copy-start = (bf16[1,4,8,48,128]{4,3,2,1,0:T(8,128)(2,1)S(1)}, bf16[1,4,8,48,128]{4,3,2,1,0:T(8,128)(2,1)}, u32[]{:S(2)}) copy-start(bf16[1,4,8,48,128]{4,3,2,1,0:T(8,128)(2,1)} %param.9) | copy-start | bytes 1179652
  0.0 2.9 %copy-start.4 = (f32[128]{0:T(128)S(1)}, f32[128]{0:T(128)}, u32[]{:S(2)}) copy-start(f32[128]{0:T(128)} %param.10) | copy-start | bytes 1540
  0.0 2.9 %copy-start.3 = (f32[128]{0:T(128)S(1)}, f32[128]{0:T(128)}, u32[]{:S(2)}) copy-start(f32[128]{0:T(128)} %param.11) | copy-start | bytes 1540
  3.4 48.2 %copy-start.2 = (bf16[3,3,3,128,128]{4,3,2,1,0:T(8,128)(2,1)S(1)}, bf16[3,3,3,128,128]{4,3,2,1,0:T(8,128)(2,1)}, u32[]{:S(2)}) copy-start(bf16[3,3,3,128,128]{4,3,2,1,0:T(8,128)(2,1)} %param.12) | copy-start | bytes 2654212
  3.5 45.5 %collective-permute-start = (bf16[2,8,48,128]{3,2,1,0:T(8,128)(2,1)S(1)}, bf16[2,8,48,128]{3,2,1,0:T(8,128)(2,1)S(1)}, u32[]{:S(2)}, u32[]{:S(2)}) collective-permute-start(bf16[2,8,48,128]{3,2,1,0:T(8,128)(2,1)S(1)} %slice.495), channel_id=1, source_target_pairs={{0,2},{2,4},{4,6},{6,8},{8,10},{10,12},{12,14},{1,3},{3,5},{5,7},{... | collective-permute-start | bytes 589832 | tf_op jit(solution)/shard_map/ppermute | solution.py:10
  49.0 3.3 %collective-permute-start.1 = (bf16[6,1,48,128]{3,2,1,0:T(8,128)(2,1)S(1)}, bf16[6,1,48,128]{3,2,1,0:T(8,128)(2,1)S(1)}, u32[]{:S(2)}, u32[]{:S(2)}) collective-permute-start(bf16[6,1,48,128]{3,2,1,0:T(8,128)(2,1)S(1)} %get-tuple-element.7), channel_id=1, source_target_pairs={{0,16},{16,32},{32,48},{48,64},{64,80},{80,96},{96,112},{112,128},... | collective-permute-start | bytes 221192 | tf_op jit(solution)/shard_map/ppermute | solution.py:21
  50.3 6.3 %collective-permute-start.2 = (bf16[6,1,48,128]{3,2,1,0:T(8,128)(2,1)S(1)}, bf16[6,1,48,128]{3,2,1,0:T(8,128)(2,1)S(1)}, u32[]{:S(2)}, u32[]{:S(2)}) collective-permute-start(bf16[6,1,48,128]{3,2,1,0:T(8,128)(2,1)S(1)} %get-tuple-element.8), channel_id=1, source_target_pairs={{16,0},{32,16},{48,32},{64,48},{80,64},{96,80},{112,96},{128,112},... | collective-permute-start | bytes 221192 | tf_op jit(solution)/shard_map/ppermute | solution.py:23
  63.2 0.7 copy-start.5
  64.3 0.7 copy-start.6
  64.3 0.7 copy-start.7
  65.5 10.9 %copy-start.1 = (bf16[3,3,3,128,128]{4,3,2,1,0:T(8,128)(2,1)S(1)}, bf16[3,3,3,128,128]{4,3,2,1,0:T(8,128)(2,1)}, u32[]{:S(2)}) copy-start(bf16[3,3,3,128,128]{4,3,2,1,0:T(8,128)(2,1)} %param.16) | copy-start | bytes 2654212
  65.5 7.7 %collective-permute-start.3 = (bf16[2,8,48,128]{3,2,1,0:T(8,128)(2,1)S(1)}, bf16[2,8,48,128]{3,2,1,0:T(8,128)(2,1)S(1)}, u32[]{:S(2)}, u32[]{:S(2)}) collective-permute-start(bf16[2,8,48,128]{3,2,1,0:T(8,128)(2,1)S(1)} %slice.515), channel_id=1, source_target_pairs={{0,2},{2,4},{4,6},{6,8},{8,10},{10,12},{12,14},{1,3},{3,5},{5,7},{... | collective-permute-start | bytes 589832 | tf_op jit(solution)/shard_map/ppermute | solution.py:10
  73.3 3.6 %collective-permute-start.4 = (bf16[6,1,48,128]{3,2,1,0:T(8,128)(2,1)S(1)}, bf16[6,1,48,128]{3,2,1,0:T(8,128)(2,1)S(1)}, u32[]{:S(2)}, u32[]{:S(2)}) collective-permute-start(bf16[6,1,48,128]{3,2,1,0:T(8,128)(2,1)S(1)} %get-tuple-element.5), channel_id=1, source_target_pairs={{0,16},{16,32},{32,48},{48,64},{64,80},{80,96},{96,112},{112,128},... | collective-permute-start | bytes 221192 | tf_op jit(solution)/shard_map/ppermute | solution.py:21
  74.9 6.3 %collective-permute-start.5 = (bf16[6,1,48,128]{3,2,1,0:T(8,128)(2,1)S(1)}, bf16[6,1,48,128]{3,2,1,0:T(8,128)(2,1)S(1)}, u32[]{:S(2)}, u32[]{:S(2)}) collective-permute-start(bf16[6,1,48,128]{3,2,1,0:T(8,128)(2,1)S(1)} %get-tuple-element.6), channel_id=1, source_target_pairs={{16,0},{32,16},{48,32},{64,48},{80,64},{96,80},{112,96},{128,112},... | collective-permute-start | bytes 221192 | tf_op jit(solution)/shard_map/ppermute | solution.py:23
  87.7 0.7 copy-start.8
where the time goes:
time: 89.8 us; the launch traced here: 89.4 us
  waiting for transfers between devices  56.2 us (63%)
  matrix products  15.3 us (17%)
  starting transfers between devices  11.5 us (13%)
  other arithmetic  5.16 us (6%)
    ppermute x2, waiting for transfers between devices, from_behind(): return lax.ppermute(shard, axis, pairs)  47.4 us
    dot_general x54, matrix products, conv_valid(): jnp.einsum('fhwc,cd->fhwd', window, weight[step_t, step_h, step_w], prefe...  15.3 us
    ppermute x2, waiting for transfers between devices, padded_2(): lax.ppermute(head, axis, [((i + 1) % count, i) for i in range(ends)])  8.63 us
    ppermute x2, starting transfers between devices, from_behind(): return lax.ppermute(shard, axis, pairs)  5.78 us
    ppermute x2, starting transfers between devices, padded_2(): lax.ppermute(tail, axis, [(i, (i + 1) % count) for i in range(ends)])  2.9 us
    ppermute x2, starting transfers between devices, padded_2(): lax.ppermute(head, axis, [((i + 1) % count, i) for i in range(ends)])  2.8 us
    reduce_sum x2, other arithmetic, activate(): spread = jnp.mean(centred * centred, axis=-1, keepdims=True)  2.01 us
  transfers between devices with their start and end apart: 6, of which 5 were waited for; matrix products, arithmetic and copies ran while one was open for 1% of the time, Pallas kernels for 0%

commit v1 on v0

v1 whole, which is shorter than its diff:
```python
import jax
import jax.numpy as jnp
from jax import lax
from jax.experimental import pallas as pl
from jax.experimental.pallas import tpu as pltpu
from jax.sharding import PartitionSpec as P

EPS = 1e-06


def activate(values, gain, shift):
    middle = jnp.mean(values, axis=-1, keepdims=True)
    centred = values - middle
    spread = jnp.mean(centred * centred, axis=-1, keepdims=True)
    normed = centred * lax.rsqrt(spread + EPS) * gain + shift
    return normed * (0.5 + 0.5 * jnp.tanh(0.5 * normed))


def put_shifted(ref, frame, pair, half, rows):
    width, channels = rows.shape
    column = lax.broadcasted_iota(jnp.int32, rows.shape, 0)
    before = jnp.where(column == 0, 0.0, pltpu.roll(rows, 1, 0))
    after = jnp.where(column == width - 1, 0.0, pltpu.roll(rows, width - 1, 0))
    lanes = pl.ds(half * channels, channels)
    ref[0, frame, pair, :, lanes] = before.astype(ref.dtype)
    ref[1, frame, pair, :, lanes] = rows.astype(ref.dtype)
    ref[2, frame, pair, :, lanes] = after.astype(ref.dtype)


def pair_taps(weight_ref, step_t, step_w):
    top, mid, low = (weight_ref[step_t, i, step_w] for i in range(3))
    none = jnp.zeros_like(top)
    upper = jnp.concatenate([jnp.concatenate([top, none], 1), jnp.concatenate([mid, top], 1)], 0)
    lower = jnp.concatenate([jnp.concatenate([low, mid], 1), jnp.concatenate([none, low], 1)], 0)
    return upper, lower


def conv_pairs(maps_ref, weight_ref, frames_of, pairs):
    width, lanes = maps_ref.shape[3:]
    total = None
    for step_w in range(3):
        for step_t in range(3):
            upper, lower = pair_taps(weight_ref, step_t, step_w)
            for rhs, skip in ((upper, 0), (lower, 1)):
                lhs = jnp.concatenate(
                    [maps_ref[step_w, f, skip : skip + pairs].reshape(pairs * width, lanes) for f in frames_of[step_t]], 0
                )
                part = jnp.dot(lhs, rhs, preferred_element_type=jnp.float32)
                total = part if total is None else total + part
    return total


def block_kernel(
    flags, video, behind, above, below, behind_above, behind_below,
    gain1, shift1, weight1, bias1, gain2, shift2, weight2, bias2, out, first, second,
):
    frames, rows, width, channels = video.shape
    is_start, has_above, has_below = flags[0] == 1, flags[1] == 1, flags[2] == 1
    inner = rows // 2

    def enter(ref, frame, row, to_frame, pair, valid):
        for half in range(2):
            values = activate(ref[frame, row + half].astype(jnp.float32), gain1[...], shift1[...])
            if valid is not None:
                values = jnp.where(valid, values, 0.0)
            put_shifted(first, to_frame, pair, half, values)

    def enter_frame(frame, carry):
        for ref, upper, lower, to in (
            (behind, behind_above, behind_below, frame),
            (video, above, below, frame + frames),
        ):
            enter(upper, frame, 0, to, 0, has_above)
            for k in range(inner):
                enter(ref, frame, 2 * k, to, k + 1, None)
            enter(lower, frame, 0, to, inner + 1, has_below)
        return carry

    lax.fori_loop(0, frames, enter_frame, 0)

    floor1 = jnp.where(is_start, frames, 0)
    floor2 = jnp.where(is_start, 2, 0)

    def layer1(step, carry):
        at = [2 * step, 2 * step + 1]
        frames_of = [[jnp.maximum(f + dt, floor1) for f in at] for dt in range(3)]
        total = conv_pairs(first, weight1, frames_of, inner + 1)
        total = total.reshape(2, inner + 1, width, 2 * channels)
        for i in range(2):
            for pair in range(inner + 1):
                for half in range(2):
                    values = total[i, pair, :, half * channels : (half + 1) * channels] + bias1[...]
                    values = activate(values, gain2[...], shift2[...])
                    if pair == 0 and half == 0:
                        values = jnp.where(has_above, values, 0.0)
                    if pair == inner and half == 1:
                        values = jnp.where(has_below, values, 0.0)
                    put_shifted(second, at[i], pair, half, values)
        return carry

    lax.fori_loop(0, (frames + 2) // 2, layer1, 0)

    def layer2(step, carry):
        at = [2 * step, 2 * step + 1]
        frames_of = [[jnp.maximum(f + dt, floor2) for f in at] for dt in range(3)]
        total = conv_pairs(second, weight2, frames_of, inner)
        total = total.reshape(2, inner, width, 2 * channels)
        for i in range(2):
            for pair in range(inner):
                for half in range(2):
                    values = total[i, pair, :, half * channels : (half + 1) * channels] + bias2[...]
                    row = 2 * pair + half
                    out[at[i], row] = (video[at[i], row].astype(jnp.float32) + values).astype(out.dtype)
        return carry

    lax.fori_loop(0, frames // 2, layer2, 0)


def body(
    video,
    norm1_gain,
    norm1_shift,
    conv1_weight,
    conv1_bias,
    norm2_gain,
    norm2_shift,
    conv2_weight,
    conv2_bias,
):
    clip = video[0]
    frames, rows, width, channels = clip.shape
    spans, slabs = lax.axis_size("ta"), lax.axis_size("ha")
    span, slab = lax.axis_index("ta"), lax.axis_index("ha")
    top, bottom = clip[:, :2], clip[:, rows - 2 :]

    def at(h, t):
        return h * spans + t

    behind = lax.ppermute(clip, "ta", [(t, t + 1) for t in range(spans - 1)])
    above = lax.ppermute(bottom, "ha", [(h, h + 1) for h in range(slabs - 1)])
    below = lax.ppermute(top, "ha", [(h + 1, h) for h in range(slabs - 1)])
    behind_above = lax.ppermute(
        bottom, ("ha", "ta"), [(at(h, t), at(h + 1, t + 1)) for h in range(slabs - 1) for t in range(spans - 1)]
    )
    behind_below = lax.ppermute(
        top, ("ha", "ta"), [(at(h + 1, t), at(h, t + 1)) for h in range(slabs - 1) for t in range(spans - 1)]
    )
    flags = jnp.stack([span == 0, slab > 0, slab < slabs - 1]).astype(jnp.int32)

    vmem = pl.BlockSpec(memory_space=pltpu.VMEM)
    vector = lambda v: v.reshape(1, channels)
    out = pl.pallas_call(
        block_kernel,
        out_shape=jax.ShapeDtypeStruct(clip.shape, clip.dtype),
        in_specs=[pl.BlockSpec(memory_space=pltpu.SMEM)] + [vmem] * 14,
        out_specs=vmem,
        scratch_shapes=[
            pltpu.VMEM((3, 2 * frames, rows // 2 + 2, width, 2 * channels), jnp.bfloat16),
            pltpu.VMEM((3, frames + 2, rows // 2 + 1, width, 2 * channels), jnp.bfloat16),
        ],
        compiler_params=pltpu.CompilerParams(vmem_limit_bytes=40 * 1024 * 1024),
        cost_estimate=pl.CostEstimate(flops=8 * 10**9, bytes_accessed=4 * 10**6, transcendentals=0),
        name="block",
    )(
        flags, clip, behind, above, below, behind_above, behind_below,
        vector(norm1_gain), vector(norm1_shift), conv1_weight, vector(conv1_bias),
        vector(norm2_gain), vector(norm2_shift), conv2_weight, vector(conv2_bias),
    )
    return out[None]


def solution(mesh):
    placed = (P(("grp", "cam"), "ta", "ha", None, None), P(), P(), P(), P(), P(), P(), P(), P())
    return jax.shard_map(
        body,
        mesh=mesh,
        in_specs=placed,
        out_specs=P(("grp", "cam"), "ta", "ha", None, None),
        check_vma=False,
    )
```

time: 89.8 us -> 67.8 us (0.76)
  the two profiles are of different devices: /device:TPU:66 before, /device:TPU:192 now
where the time goes in v1:
time: 67.8 us; the launch traced here: 67.4 us
  starting transfers between devices  45.3 us (67%)
  Pallas kernels  13.5 us (20%)
  waiting for transfers between devices  4.5 us (7%)
  local copies, waits for them, and re-layouts  3.99 us (6%)
    ppermute x1, starting transfers between devices, body(): below = lax.ppermute(top, 'ha', [(h + 1, h) for h in range(slabs - 1)])  37 us
    pallas_call x1, Pallas kernels, body(): pl.pallas_call(block_kernel, out_shape=jax.ShapeDtypeStruct(clip.shape, c...  13.5 us
    ppermute x1, waiting for transfers between devices, body(): above = lax.ppermute(bottom, 'ha', [(h, h + 1) for h in range(slabs - 1)])  4.35 us
    ppermute x1, starting transfers between devices, body(): behind = lax.ppermute(clip, 'ta', [(t, t + 1) for t in range(spans - 1)])  3.7 us
    unnamed x18, local copies, waits for them, and re-layouts  3.03 us
    ppermute x1, starting transfers between devices, body(): above = lax.ppermute(bottom, 'ha', [(h, h + 1) for h in range(slabs - 1)])  1.95 us
  transfers between devices with their start and end apart: 5, of which 2 were waited for; matrix products, arithmetic and copies ran while one was open for 2% of the time, Pallas kernels for 0%

profile of v1, /device:TPU:192, one launch (start us, length us, event | category | flops | bytes accessed | tf_op | source)
XLA Modules:
  0.0 67.4 jit_solution(2338170822312756955)
XLA Ops:
  0.0 0.0 copy-start
  0.0 3.7 %collective-permute-start = (bf16[4,8,48,128]{3,2,1,0:T(8,128)(2,1)}, bf16[4,8,48,128]{3,2,1,0:T(8,128)(2,1)S(1)}, u32[]{:S(2)}, u32[]{:S(2)}) collective-permute-start(bf16[4,8,48,128]{3,2,1,0:T(8,128)(2,1)} %bitcast.11), channel_id=1, source_target_pairs={{0,2},{2,4},{4,6},{6,8},{8,10},{10,12},{12,14},{1,3},{3,5},{5,7},{... | collective-permute-start | bytes 1179656 | tf_op jit(solution)/shard_map/ppermute | solution.py:139
  3.7 1.0 %fusion = (bf16[4,2,48,128]{3,2,1,0:T(8,128)(2,1)S(1)}, bf16[4,2,48,128]{3,2,1,0:T(8,128)(2,1)S(1)}) fusion(bf16[4,8,48,128]{3,2,1,0:T(8,128)(2,1)} %bitcast.12), kind=kLoop, calls=%fused_computation.1 | loop fusion | bytes 393216 | tf_op jit(solution)/shard_map/slice | solution.py:134
  4.7 1.3 %collective-permute-start.4 = (bf16[4,2,48,128]{3,2,1,0:T(8,128)(2,1)S(1)}, bf16[4,2,48,128]{3,2,1,0:T(8,128)(2,1)S(1)}, u32[]{:S(2)}, u32[]{:S(2)}) collective-permute-start(bf16[4,2,48,128]{3,2,1,0:T(8,128)(2,1)S(1)} %get-tuple-element.5), channel_id=1, source_target_pairs={{16,2},{18,4},{20,6},{22,8},{24,10},{26,12},{28,14},{32,18},{34,20... | collective-permute-start | bytes 294920 | tf_op jit(solution)/shard_map/ppermute | solution.py:145
  6.0 37.0 %collective-permute-start.2 = (bf16[4,2,48,128]{3,2,1,0:T(8,128)(2,1)S(1)}, bf16[4,2,48,128]{3,2,1,0:T(8,128)(2,1)S(1)}, u32[]{:S(2)}, u32[]{:S(2)}) collective-permute-start(bf16[4,2,48,128]{3,2,1,0:T(8,128)(2,1)S(1)} %get-tuple-element.5), channel_id=1, source_target_pairs={{16,0},{32,16},{48,32},{64,48},{80,64},{96,80},{112,96},{128,112},... | collective-permute-start | bytes 294920 | tf_op jit(solution)/shard_map/ppermute | solution.py:141
  43.0 1.3 %collective-permute-start.3 = (bf16[4,2,48,128]{3,2,1,0:T(8,128)(2,1)S(1)}, bf16[4,2,48,128]{3,2,1,0:T(8,128)(2,1)S(1)}, u32[]{:S(2)}, u32[]{:S(2)}) collective-permute-start(bf16[4,2,48,128]{3,2,1,0:T(8,128)(2,1)S(1)} %get-tuple-element.6), channel_id=1, source_target_pairs={{0,18},{2,20},{4,22},{6,24},{8,26},{10,28},{12,30},{16,34},{18,36}... | collective-permute-start | bytes 294920 | tf_op jit(solution)/shard_map/ppermute | solution.py:142
  44.3 2.0 %collective-permute-start.1 = (bf16[4,2,48,128]{3,2,1,0:T(8,128)(2,1)S(1)}, bf16[4,2,48,128]{3,2,1,0:T(8,128)(2,1)S(1)}, u32[]{:S(2)}, u32[]{:S(2)}) collective-permute-start(bf16[4,2,48,128]{3,2,1,0:T(8,128)(2,1)S(1)} %get-tuple-element.6), channel_id=1, source_target_pairs={{0,16},{16,32},{32,48},{48,64},{64,80},{80,96},{96,112},{112,128},... | collective-permute-start | bytes 294920 | tf_op jit(solution)/shard_map/ppermute | solution.py:140
  46.3 0.1 add_convert_fusion.flags
  46.3 0.0 collective-permute-done.4.behind_below
  46.4 0.0 collective-permute-done.2.below
  46.4 0.1 collective-permute-done.3.behind_above
  46.5 4.3 %collective-permute-done.1.above = bf16[4,2,48,128]{3,2,1,0:T(8,128)(2,1)S(1)} collective-permute-done((bf16[4,2,48,128]{3,2,1,0:T(8,128)(2,1)S(1)}, bf16[4,2,48,128]{3,2,1,0:T(8,128)(2,1)S(1)}, u32[]{:S(2)}, u32[]{:S(2)}) %collective-permute-start.1) | collective-permute-done | bytes 98336 | tf_op jit(solution)/shard_map/ppermute | solution.py:140
  50.8 0.0 collective-permute-done.behind
  50.8 0.0 copy-start.6
  50.9 0.0 copy-start.7
  50.9 0.0 copy-start.8
  50.9 0.0 copy-start.3
  50.9 0.0 copy-start.4
  50.9 0.0 copy-start.5
  50.9 0.0 copy-done
  50.9 0.6 copy-done.6
  51.5 0.0 copy-done.7
  51.5 0.0 copy-done.8
  51.5 0.0 copy-done.3
  51.6 0.0 copy-done.4
  51.6 0.0 copy-done.5
  51.6 0.0 copy-start.1
  51.6 1.2 %copy-done.1 = bf16[3,3,3,128,128]{4,3,2,1,0:T(8,128)(2,1)S(1)} copy-done((bf16[3,3,3,128,128]{4,3,2,1,0:T(8,128)(2,1)S(1)}, bf16[3,3,3,128,128]{4,3,2,1,0:T(8,128)(2,1)}, u32[]{:S(2)}) %copy-start.1) | copy-done | bytes 884760
  52.8 0.0 copy-start.2
  52.8 1.2 %copy-done.2 = bf16[3,3,3,128,128]{4,3,2,1,0:T(8,128)(2,1)S(1)} copy-done((bf16[3,3,3,128,128]{4,3,2,1,0:T(8,128)(2,1)S(1)}, bf16[3,3,3,128,128]{4,3,2,1,0:T(8,128)(2,1)}, u32[]{:S(2)}) %copy-start.2) | copy-done | bytes 884760
  53.9 13.5 %block.1 = bf16[4,8,48,128]{3,2,1,0:T(8,128)(2,1)} custom-call(s32[3]{0:T(128)S(1)} %add_convert_fusion.flags, bf16[4,8,48,128]{3,2,1,0:T(8,128)(2,1)S(1)} %bitcast.13, bf16[4,8,48,128]{3,2,1,0:T(8,128)(2,1)S(1)} %collective-permute-done.behind, bf16[4,2,48,128]{3,2,1,0:T(8,128)(2,1)S(1)} %collective-permute-done.1.above, ...), custom_call_target="tpu_custom_call" | custom-call | flops 8000000000 | bytes 4000000 | tf_op jit(solution)/shard_map/block/pallas_call | solution.py:152
Async XLA Ops:
  0.0 50.9 %copy-start = (bf16[1,4,8,48,128]{4,3,2,1,0:T(8,128)(2,1)S(1)}, bf16[1,4,8,48,128]{4,3,2,1,0:T(8,128)(2,1)}, u32[]{:S(2)}) copy-start(bf16[1,4,8,48,128]{4,3,2,1,0:T(8,128)(2,1)} %param.9) | copy-start | bytes 1179652
  0.0 50.8 %collective-permute-start = (bf16[4,8,48,128]{3,2,1,0:T(8,128)(2,1)}, bf16[4,8,48,128]{3,2,1,0:T(8,128)(2,1)S(1)}, u32[]{:S(2)}, u32[]{:S(2)}) collective-permute-start(bf16[4,8,48,128]{3,2,1,0:T(8,128)(2,1)} %bitcast.11), channel_id=1, source_target_pairs={{0,2},{2,4},{4,6},{6,8},{8,10},{10,12},{12,14},{1,3},{3,5},{5,7},{... | collective-permute-start | bytes 1179656 | tf_op jit(solution)/shard_map/ppermute | solution.py:139
  4.7 41.7 %collective-permute-start.4 = (bf16[4,2,48,128]{3,2,1,0:T(8,128)(2,1)S(1)}, bf16[4,2,48,128]{3,2,1,0:T(8,128)(2,1)S(1)}, u32[]{:S(2)}, u32[]{:S(2)}) collective-permute-start(bf16[4,2,48,128]{3,2,1,0:T(8,128)(2,1)S(1)} %get-tuple-element.5), channel_id=1, source_target_pairs={{16,2},{18,4},{20,6},{22,8},{24,10},{26,12},{28,14},{32,18},{34,20... | collective-permute-start | bytes 294920 | tf_op jit(solution)/shard_map/ppermute | solution.py:145
  6.0 40.4 %collective-permute-start.2 = (bf16[4,2,48,128]{3,2,1,0:T(8,128)(2,1)S(1)}, bf16[4,2,48,128]{3,2,1,0:T(8,128)(2,1)S(1)}, u32[]{:S(2)}, u32[]{:S(2)}) collective-permute-start(bf16[4,2,48,128]{3,2,1,0:T(8,128)(2,1)S(1)} %get-tuple-element.5), channel_id=1, source_target_pairs={{16,0},{32,16},{48,32},{64,48},{80,64},{96,80},{112,96},{128,112},... | collective-permute-start | bytes 294920 | tf_op jit(solution)/shard_map/ppermute | solution.py:141
  43.0 3.5 %collective-permute-start.3 = (bf16[4,2,48,128]{3,2,1,0:T(8,128)(2,1)S(1)}, bf16[4,2,48,128]{3,2,1,0:T(8,128)(2,1)S(1)}, u32[]{:S(2)}, u32[]{:S(2)}) collective-permute-start(bf16[4,2,48,128]{3,2,1,0:T(8,128)(2,1)S(1)} %get-tuple-element.6), channel_id=1, source_target_pairs={{0,18},{2,20},{4,22},{6,24},{8,26},{10,28},{12,30},{16,34},{18,36}... | collective-permute-start | bytes 294920 | tf_op jit(solution)/shard_map/ppermute | solution.py:142
  44.3 6.5 %collective-permute-start.1 = (bf16[4,2,48,128]{3,2,1,0:T(8,128)(2,1)S(1)}, bf16[4,2,48,128]{3,2,1,0:T(8,128)(2,1)S(1)}, u32[]{:S(2)}, u32[]{:S(2)}) collective-permute-start(bf16[4,2,48,128]{3,2,1,0:T(8,128)(2,1)S(1)} %get-tuple-element.6), channel_id=1, source_target_pairs={{0,16},{16,32},{32,48},{48,64},{64,80},{80,96},{96,112},{112,128},... | collective-permute-start | bytes 294920 | tf_op jit(solution)/shard_map/ppermute | solution.py:140
  50.8 0.7 copy-start.6
  50.9 0.7 copy-start.7
  50.9 0.7 %copy-start.8 = (f32[128]{0:T(128)S(1)}, f32[128]{0:T(128)}, u32[]{:S(2)}) copy-start(f32[128]{0:T(128)} %param.17) | copy-start | bytes 1540
  50.9 0.7 %copy-start.3 = (f32[128]{0:T(128)S(1)}, f32[128]{0:T(128)}, u32[]{:S(2)}) copy-start(f32[128]{0:T(128)} %param.10) | copy-start | bytes 1540
  50.9 0.7 %copy-start.4 = (f32[128]{0:T(128)S(1)}, f32[128]{0:T(128)}, u32[]{:S(2)}) copy-start(f32[128]{0:T(128)} %param.11) | copy-start | bytes 1540
  50.9 0.7 %copy-start.5 = (f32[128]{0:T(128)S(1)}, f32[128]{0:T(128)}, u32[]{:S(2)}) copy-start(f32[128]{0:T(128)} %param.13) | copy-start | bytes 1540
  51.6 1.2 %copy-start.1 = (bf16[3,3,3,128,128]{4,3,2,1,0:T(8,128)(2,1)S(1)}, bf16[3,3,3,128,128]{4,3,2,1,0:T(8,128)(2,1)}, u32[]{:S(2)}) copy-start(bf16[3,3,3,128,128]{4,3,2,1,0:T(8,128)(2,1)} %weight1.1) | copy-start | bytes 2654212
  52.8 1.2 %copy-start.2 = (bf16[3,3,3,128,128]{4,3,2,1,0:T(8,128)(2,1)S(1)}, bf16[3,3,3,128,128]{4,3,2,1,0:T(8,128)(2,1)}, u32[]{:S(2)}) copy-start(bf16[3,3,3,128,128]{4,3,2,1,0:T(8,128)(2,1)} %weight2.1) | copy-start | bytes 2654212

commit v2 on v0

v2 whole, which is shorter than its diff:
```python
import jax
import jax.numpy as jnp
from jax import lax
from jax.experimental import pallas as pl
from jax.experimental.pallas import tpu as pltpu
from jax.sharding import PartitionSpec as P


EPS = 1e-06
PAD = 8


def activate(values, gain, shift):
    middle = jnp.mean(values, axis=-1, keepdims=True)
    centred = values - middle
    spread = jnp.mean(centred * centred, axis=-1, keepdims=True)
    half = centred * lax.rsqrt(spread + EPS) * gain + shift
    return half + half * jnp.tanh(half)


def put_shifted(ref, frame, row, slot, values):
    width = values.shape[0]
    slot[PAD : PAD + width] = values
    ref[0, frame, row] = slot[PAD - 1 : PAD - 1 + width].astype(ref.dtype)
    ref[1, frame, row] = values.astype(ref.dtype)
    ref[2, frame, row] = slot[PAD + 1 : PAD + 1 + width].astype(ref.dtype)


def clear_slots(slots):
    for slot in range(slots.shape[0]):
        slots[slot, :PAD] = jnp.zeros((PAD, slots.shape[2]), slots.dtype)
        slots[slot, slots.shape[1] - PAD :] = jnp.zeros((PAD, slots.shape[2]), slots.dtype)


def pair_taps(weight_ref, step_t, step_w):
    top, mid, low = (weight_ref[step_t, i, step_w] for i in range(3))
    none = jnp.zeros_like(top)
    upper = jnp.concatenate([jnp.concatenate([top, none], 1), jnp.concatenate([mid, top], 1)], 0)
    lower = jnp.concatenate([jnp.concatenate([low, mid], 1), jnp.concatenate([none, low], 1)], 0)
    return upper, lower


def conv_pairs(maps_ref, weight_ref, taps, pairs):
    total = None
    for step_t, frame in taps:
        for step_w in range(3):
            for skip, rhs in enumerate(pair_taps(weight_ref, step_t, step_w)):
                rows = [2 * (skip + k) for k in range(pairs)]
                left = jnp.concatenate([maps_ref[step_w, frame, r] for r in rows], 0)
                right = jnp.concatenate([maps_ref[step_w, frame, r + 1] for r in rows], 0)
                lhs = jnp.concatenate([left, right], 1)
                part = jnp.dot(lhs, rhs, preferred_element_type=jnp.float32)
                total = part if total is None else total + part
    return total


def pick(total, row, width, channels):
    pair, half = divmod(row, 2)
    return total[pair * width : (pair + 1) * width, half * channels : (half + 1) * channels]


def ready_kernel(video, gain1, shift1, bias1, gain2, shift2, bias2, top, bottom, table, rows_in, sems):
    rows = video.shape[1]
    vectors = (gain1, shift1, bias1, gain2, shift2, bias2)
    loads = [
        pltpu.make_async_copy(video.at[:, :2], top, sems.at[0]),
        pltpu.make_async_copy(video.at[:, rows - 2 :], bottom, sems.at[1]),
    ] + [pltpu.make_async_copy(v, rows_in.at[i], sems.at[2 + i]) for i, v in enumerate(vectors)]
    for load in loads:
        load.start()
    for load in loads:
        load.wait()
    for i in range(len(vectors)):
        table[i] = rows_in[i] * (1.0 if i in (2, 5) else 0.5)


def near_kernel(
    flags, video, above, below, table, weight1_hbm, weight2_hbm,
    part1, part2, weight1, weight2, first, second, slots, sems,
):
    frames, rows, width, channels = video.shape
    loads = [
        pltpu.make_async_copy(weight1_hbm, weight1, sems.at[0]),
        pltpu.make_async_copy(weight2_hbm, weight2, sems.at[1]),
    ]
    for load in loads:
        load.start()
    clear_slots(slots)
    has_above, has_below = flags[1] == 1, flags[2] == 1
    g1, s1, b1, g2, s2, _ = (table[i] for i in range(6))

    def enter(frame):
        for row in range(-2, rows + 2):
            ref, at = (above, row + 2) if row < 0 else (below, row - rows) if row >= rows else (video, row)
            values = activate(ref[frame, at].astype(jnp.float32), g1, s1)
            if row < 0:
                values = jnp.where(has_above, values, 0.0)
            if row >= rows:
                values = jnp.where(has_below, values, 0.0)
            put_shifted(first, frame, row + 2, slots.at[frame * (rows + 4) + row + 2], values)

    def middle(total, to):
        for row in range(rows + 2):
            values = activate(pick(total, row, width, channels) + b1, g2, s2)
            if row == 0:
                values = jnp.where(has_above, values, 0.0)
            if row == rows + 1:
                values = jnp.where(has_below, values, 0.0)
            put_shifted(second, to, row, slots.at[(frames + to) * (rows + 4) + row], values)

    half = rows // 2
    enter(0)
    loads[0].wait()
    part1[0] = conv_pairs(first, weight1, [(2, 0)], half + 1)
    enter(1)
    part1[1] = conv_pairs(first, weight1, [(1, 0), (2, 1)], half + 1)
    enter(2)
    middle(conv_pairs(first, weight1, [(0, 0), (1, 1), (2, 2)], half + 1), 0)
    enter(3)
    middle(conv_pairs(first, weight1, [(0, 1), (1, 2), (2, 3)], half + 1), 1)
    loads[1].wait()
    part2[0] = conv_pairs(second, weight2, [(2, 0)], half)
    part2[1] = conv_pairs(second, weight2, [(1, 0), (2, 1)], half)


def far_kernel(
    flags, video, above, below, behind, behind_above, behind_below, part1, part2,
    table, weight1, weight2, out, first, second, slots,
):
    frames, rows, width, channels = video.shape
    clear_slots(slots)
    is_start, has_above, has_below = flags[0] == 1, flags[1] == 1, flags[2] == 1
    g1, s1, b1, g2, s2, b2 = (table[i] for i in range(6))

    def enter(frame):
        for row in range(-2, rows + 2):
            at = row + 2 if row < 0 else row - rows if row >= rows else row
            ref, own = (behind_above, above) if row < 0 else (behind_below, below) if row >= rows else (behind, video)
            values = ref[frame, at]
            if frame >= frames - 2:
                values = jnp.where(is_start, own[0, at], values)
            values = activate(values.astype(jnp.float32), g1, s1)
            if row < 0:
                values = jnp.where(has_above, values, 0.0)
            if row >= rows:
                values = jnp.where(has_below, values, 0.0)
            put_shifted(first, frame, row + 2, slots.at[frame * (rows + 4) + row + 2], values)

    def middle(total, to):
        for row in range(rows + 2):
            values = activate(pick(total, row, width, channels) + b1, g2, s2)
            if row == 0:
                values = jnp.where(has_above, values, 0.0)
            if row == rows + 1:
                values = jnp.where(has_below, values, 0.0)
            put_shifted(second, to, row, slots.at[(frames + to) * (rows + 4) + row], values)
            if to < 2:
                for step_w in range(3):
                    second[step_w, to, row] = jnp.where(is_start, second[step_w, 2, row], second[step_w, to, row])

    def leave(total, frame):
        for row in range(rows):
            values = pick(total, row, width, channels) + b2
            out[frame, row] = (video[frame, row].astype(jnp.float32) + values).astype(out.dtype)

    half = rows // 2
    enter(3)
    total = conv_pairs(first, weight1, [(0, 3)], half + 1) + part1[1]
    enter(2)
    middle(total, 3)
    total = conv_pairs(first, weight1, [(0, 2), (1, 3)], half + 1) + part1[0]
    enter(1)
    middle(total, 2)
    total = conv_pairs(first, weight1, [(0, 1), (1, 2), (2, 3)], half + 1)
    enter(0)
    middle(total, 1)
    total = conv_pairs(first, weight1, [(0, 0), (1, 1), (2, 2)], half + 1)
    leave(conv_pairs(second, weight2, [(0, 3)], half) + part2[1], 3)
    leave(conv_pairs(second, weight2, [(0, 2), (1, 3)], half) + part2[0], 2)
    middle(total, 0)
    leave(conv_pairs(second, weight2, [(0, 1), (1, 2), (2, 3)], half), 1)
    leave(conv_pairs(second, weight2, [(0, 0), (1, 1), (2, 2)], half), 0)


VMEM = pl.BlockSpec(memory_space=pltpu.VMEM)
SMEM = pl.BlockSpec(memory_space=pltpu.SMEM)
OUTSIDE = pl.BlockSpec(memory_space=pltpu.HBM)


def hbm(array):
    return pltpu.with_memory_space_constraint(array, pltpu.HBM)


def prepare(clip, *vectors):
    frames, _, width, channels = clip.shape
    edge = jax.ShapeDtypeStruct((frames, 2, width, channels), clip.dtype)
    return pl.pallas_call(
        ready_kernel,
        out_shape=[edge, edge, jax.ShapeDtypeStruct((6, 1, channels), jnp.float32)],
        in_specs=[OUTSIDE] * 7,
        out_specs=[VMEM] * 3,
        scratch_shapes=[pltpu.VMEM((6, 1, channels), jnp.float32), pltpu.SemaphoreType.DMA((8,))],
        compiler_params=pltpu.CompilerParams(vmem_limit_bytes=4 * 1024 * 1024),
        name="ready",
    )(hbm(clip), *(hbm(v.reshape(1, channels)) for v in vectors))


def local_block(flags, clip, behind, above, below, behind_above, behind_below, table, weight1, weight2):
    frames, rows, width, channels = clip.shape
    bf16, f32 = jnp.bfloat16, jnp.float32
    half = rows // 2
    maps = [
        pltpu.VMEM((3, frames, rows + 4, width, channels), bf16),
        pltpu.VMEM((3, frames, rows + 2, width, channels), bf16),
        pltpu.VMEM((2 * frames * (rows + 4), width + 2 * PAD, channels), f32),
    ]
    limit = pltpu.CompilerParams(vmem_limit_bytes=24 * 1024 * 1024)
    part1, part2, weight1, weight2 = pl.pallas_call(
        near_kernel,
        out_shape=[
            jax.ShapeDtypeStruct((2, (half + 1) * width, 2 * channels), f32),
            jax.ShapeDtypeStruct((2, half * width, 2 * channels), f32),
            jax.ShapeDtypeStruct(weight1.shape, bf16),
            jax.ShapeDtypeStruct(weight2.shape, bf16),
        ],
        in_specs=[SMEM] + [VMEM] * 4 + [OUTSIDE] * 2,
        out_specs=[VMEM] * 4,
        scratch_shapes=maps + [pltpu.SemaphoreType.DMA((2,))],
        compiler_params=limit,
        cost_estimate=pl.CostEstimate(flops=4 * 10**9, bytes_accessed=4 * 10**6, transcendentals=0),
        name="near",
    )(flags, clip, above, below, table, hbm(weight1), hbm(weight2))
    return pl.pallas_call(
        far_kernel,
        out_shape=jax.ShapeDtypeStruct(clip.shape, clip.dtype),
        in_specs=[SMEM] + [VMEM] * 11,
        out_specs=VMEM,
        scratch_shapes=maps,
        compiler_params=limit,
        cost_estimate=pl.CostEstimate(flops=4 * 10**9, bytes_accessed=4 * 10**6, transcendentals=0),
        name="far",
    )(
        flags, clip, above, below, behind, behind_above, behind_below, part1, part2,
        table, weight1, weight2,
    )


def body(
    video,
    norm1_gain,
    norm1_shift,
    conv1_weight,
    conv1_bias,
    norm2_gain,
    norm2_shift,
    conv2_weight,
    conv2_bias,
):
    clip = video[0]
    spans, slabs = lax.axis_size("ta"), lax.axis_size("ha")
    span, slab = lax.axis_index("ta"), lax.axis_index("ha")

    def at(h, t):
        return h * spans + t

    up = [(h, h + 1) for h in range(slabs - 1)]
    on = [(t, t + 1) for t in range(spans - 1)]

    behind = lax.ppermute(clip, "ta", on)
    top, bottom, table = prepare(clip, norm1_gain, norm1_shift, conv1_bias, norm2_gain, norm2_shift, conv2_bias)
    behind_below = lax.ppermute(top, ("ha", "ta"), [(at(h, t), at(g, n)) for g, h in up for t, n in on])
    above = lax.ppermute(bottom, "ha", up)
    behind_above = lax.ppermute(bottom, ("ha", "ta"), [(at(g, t), at(h, n)) for g, h in up for t, n in on])
    below = lax.ppermute(top, "ha", [(h, g) for g, h in up])
    flags = jnp.stack([span == 0, slab > 0, slab < slabs - 1]).astype(jnp.int32)
    out = local_block(flags, clip, behind, above, below, behind_above, behind_below, table, conv1_weight, conv2_weight)
    return out[None]


def solution(mesh):
    placed = (P(("grp", "cam"), "ta", "ha", None, None), P(), P(), P(), P(), P(), P(), P(), P())
    return jax.shard_map(
        body,
        mesh=mesh,
        in_specs=placed,
        out_specs=P(("grp", "cam"), "ta", "ha", None, None),
        check_vma=False,
    )
```

time: 89.8 us -> 59 us (0.66)
  waiting for transfers between devices: 56.2 us -> 27.2 us
  matrix products: 15.3 us -> 0 us
  Pallas kernels: 0 us -> 12.1 us
  starting transfers between devices: 11.5 us -> 19.3 us
  other arithmetic: 5.16 us -> 0.08 us
    ppermute x6 -> x5, waiting for transfers between devices: 56.2 us -> 27.2 us  [the longest x1 22.7 us: body(): behind = lax.ppermute(clip, 'ta', on)]
    dot_general x54 -> x0, matrix products: 15.3 us -> none  [conv_valid(): jnp.einsum('fhwc,cd->fhwd', window, weight[step_t, step_h, step_w], prefe...]
    pallas_call x0 -> x3, Pallas kernels: none -> 12.1 us  [the longest x1 5.54 us: local_block(): pl.pallas_call(far_kernel, out_shape=jax.ShapeDtypeStruct(clip.shape, cli...]
    ppermute x6 -> x5, starting transfers between devices: 11.5 us -> 19.3 us  [the longest x1 7.09 us: body(): lax.ppermute(bottom, ('ha', 'ta'), [(at(g, t), at(h, n)) for g, h in up f...]
    reduce_sum x3 -> x0, other arithmetic: 3.35 us -> none  [the longest x2 2.01 us: activate(): spread = jnp.mean(centred * centred, axis=-1, keepdims=True)]
    convert_element_type x2 -> x1, other arithmetic: 0.98 us -> 0.08 us  [body(): flags = jnp.stack([span == 0, slab > 0, slab < slabs - 1]).astype(jnp.int32)]
  transfers between devices with their start and end apart: 6 -> 5, of which waited for: 5 -> 2; matrix products, arithmetic and copies ran while one was open for 1% -> 0% of each run, Pallas kernels for 0% -> 9%
where the time goes in v2:
time: 59 us; the launch traced here: 58.7 us
  waiting for transfers between devices  27.2 us (46%)
  starting transfers between devices  19.3 us (33%)
  Pallas kernels  12.1 us (21%)
    ppermute x1, waiting for transfers between devices, body(): behind = lax.ppermute(clip, 'ta', on)  22.7 us
    ppermute x1, starting transfers between devices, body(): lax.ppermute(bottom, ('ha', 'ta'), [(at(g, t), at(h, n)) for g, h in up f...  7.09 us
    ppermute x1, starting transfers between devices, body(): above = lax.ppermute(bottom, 'ha', up)  6.03 us
    pallas_call x1, Pallas kernels, local_block(): pl.pallas_call(far_kernel, out_shape=jax.ShapeDtypeStruct(clip.shape, cli...  5.54 us
    pallas_call x1, Pallas kernels, local_block(): pl.pallas_call(near_kernel, out_shape=[jax.ShapeDtypeStruct((2, (half + 1...  5.45 us
    ppermute x1, waiting for transfers between devices, body(): below = lax.ppermute(top, 'ha', [(h, g) for g, h in up])  4.42 us
    ppermute x1, starting transfers between devices, body(): behind = lax.ppermute(clip, 'ta', on)  3.57 us
    ppermute x1, starting transfers between devices, body(): lax.ppermute(top, ('ha', 'ta'), [(at(h, t), at(g, n)) for g, h in up for...  1.31 us
  transfers between devices with their start and end apart: 5, of which 2 were waited for; matrix products, arithmetic and copies ran while one was open for 0% of the time, Pallas kernels for 9%

profile of v2, /device:TPU:66, one launch (start us, length us, event | category | flops | bytes accessed | tf_op | source)
XLA Modules:
  0.0 58.7 jit_solution(2315021894902452281)
XLA Ops:
  0.0 0.0 copy-start
  0.0 1.1 %ready.1 = (bf16[4,2,48,128]{3,2,1,0:T(8,128)(2,1)S(1)}, bf16[4,2,48,128]{3,2,1,0:T(8,128)(2,1)S(1)}, f32[6,1,128]{2,1,0:T(1,128)S(1)}) custom-call(bf16[4,8,48,128]{3,2,1,0:T(8,128)(2,1)} %bitcast.11, f32[1,128]{1,0:T(1,128)} %bitcast.15, f32[1,128]{1,0:T(1,128)} %bitcast.16, f32[1,128]{1,0:T(1,128)} %bitcast.17, f32[1,128]{1,0:T(1,128)} %bitcast.18, ...), custom_call_target="tpu_custom_call" | custom-call | tf_op jit(solution)/shard_map/ready/pallas_call | solution.py:197
  1.1 7.1 %collective-permute-start.3 = (bf16[4,2,48,128]{3,2,1,0:T(8,128)(2,1)S(1)}, bf16[4,2,48,128]{3,2,1,0:T(8,128)(2,1)S(1)}, u32[]{:S(2)}, u32[]{:S(2)}) collective-permute-start(bf16[4,2,48,128]{3,2,1,0:T(8,128)(2,1)S(1)} %get-tuple-element.12), channel_id=1, source_target_pairs={{0,18},{2,20},{4,22},{6,24},{8,26},{10,28},{12,30},{16,34},{18,36}... | collective-permute-start | bytes 294920 | tf_op jit(solution)/shard_map/ppermute | solution.py:273
  8.2 6.0 %collective-permute-start = (bf16[4,2,48,128]{3,2,1,0:T(8,128)(2,1)S(1)}, bf16[4,2,48,128]{3,2,1,0:T(8,128)(2,1)S(1)}, u32[]{:S(2)}, u32[]{:S(2)}) collective-permute-start(bf16[4,2,48,128]{3,2,1,0:T(8,128)(2,1)S(1)} %get-tuple-element.12), channel_id=1, source_target_pairs={{0,16},{16,32},{32,48},{48,64},{64,80},{80,96},{96,112},{112,128},... | collective-permute-start | bytes 294920 | tf_op jit(solution)/shard_map/ppermute | solution.py:272
  14.2 1.3 %collective-permute-start.4 = (bf16[4,2,48,128]{3,2,1,0:T(8,128)(2,1)S(1)}, bf16[4,2,48,128]{3,2,1,0:T(8,128)(2,1)S(1)}, u32[]{:S(2)}, u32[]{:S(2)}) collective-permute-start(bf16[4,2,48,128]{3,2,1,0:T(8,128)(2,1)S(1)} %get-tuple-element.13), channel_id=1, source_target_pairs={{16,2},{18,4},{20,6},{22,8},{24,10},{26,12},{28,14},{32,18},{34,20... | collective-permute-start | bytes 294920 | tf_op jit(solution)/shard_map/ppermute | solution.py:271
  15.5 1.3 %collective-permute-start.1 = (bf16[4,2,48,128]{3,2,1,0:T(8,128)(2,1)S(1)}, bf16[4,2,48,128]{3,2,1,0:T(8,128)(2,1)S(1)}, u32[]{:S(2)}, u32[]{:S(2)}) collective-permute-start(bf16[4,2,48,128]{3,2,1,0:T(8,128)(2,1)S(1)} %get-tuple-element.13), channel_id=1, source_target_pairs={{16,0},{32,16},{48,32},{64,48},{80,64},{96,80},{112,96},{128,112},... | collective-permute-start | bytes 294920 | tf_op jit(solution)/shard_map/ppermute | solution.py:274
  16.9 0.0 copy-done
  16.9 3.6 %collective-permute-start.2 = (bf16[4,8,48,128]{3,2,1,0:T(8,128)(2,1)S(1)}, bf16[4,8,48,128]{3,2,1,0:T(8,128)(2,1)S(1)}, u32[]{:S(2)}, u32[]{:S(2)}) collective-permute-start(bf16[4,8,48,128]{3,2,1,0:T(8,128)(2,1)S(1)} %bitcast.12), channel_id=1, source_target_pairs={{0,2},{2,4},{4,6},{6,8},{8,10},{10,12},{12,14},{1,3},{3,5},{5,7},{... | collective-permute-start | bytes 1179656 | tf_op jit(solution)/shard_map/ppermute | solution.py:269
  20.4 0.1 add_convert_fusion.flags
  20.5 0.0 collective-permute-done.above
  20.5 4.4 %collective-permute-done.1.below = bf16[4,2,48,128]{3,2,1,0:T(8,128)(2,1)S(1)} collective-permute-done((bf16[4,2,48,128]{3,2,1,0:T(8,128)(2,1)S(1)}, bf16[4,2,48,128]{3,2,1,0:T(8,128)(2,1)S(1)}, u32[]{:S(2)}, u32[]{:S(2)}) %collective-permute-start.1) | collective-permute-done | bytes 98336 | tf_op jit(solution)/shard_map/ppermute | solution.py:274
  24.9 5.5 %near.1 = (f32[2,240,256]{2,1,0:T(8,128)S(1)}, f32[2,192,256]{2,1,0:T(8,128)S(1)}, bf16[3,3,3,128,128]{4,3,2,1,0:T(8,128)(2,1)S(1)}, bf16[3,3,3,128,128]{4,3,2,1,0:T(8,128)(2,1)S(1)}) custom-call(s32[3]{0:T(128)S(1)} %add_convert_fusion.flags, bf16[4,8,48,128]{3,2,1,0:T(8,128)(2,1)S(1)} %bitcast.13, bf16[4,2,48,128]{3,2,1,0:T(8,128)(2,1)S(1)} %collective-permute-done.above, ...), custom_call_target="tpu_custom_call" | custom-call | flops 4000000000 | bytes 4000000 | tf_op jit(solution)/shard_map/near/pallas_call | solution.py:218
  30.4 0.0 collective-permute-done.3.behind_above
  30.4 0.0 collective-permute-done.4.behind_below
  30.4 22.7 %collective-permute-done.2.behind = bf16[4,8,48,128]{3,2,1,0:T(8,128)(2,1)S(1)} collective-permute-done((bf16[4,8,48,128]{3,2,1,0:T(8,128)(2,1)S(1)}, bf16[4,8,48,128]{3,2,1,0:T(8,128)(2,1)S(1)}, u32[]{:S(2)}, u32[]{:S(2)}) %collective-permute-start.2) | collective-permute-done | bytes 393248 | tf_op jit(solution)/shard_map/ppermute | solution.py:269
  53.2 5.5 %far.1 = bf16[4,8,48,128]{3,2,1,0:T(8,128)(2,1)} custom-call(s32[3]{0:T(128)S(1)} %add_convert_fusion.flags, bf16[4,8,48,128]{3,2,1,0:T(8,128)(2,1)S(1)} %bitcast.14, bf16[4,2,48,128]{3,2,1,0:T(8,128)(2,1)S(1)} %collective-permute-done.above, bf16[4,2,48,128]{3,2,1,0:T(8,128)(2,1)S(1)} %collective-permute-done.1.below, ...), custom_call_target="tpu_custom_call" | custom-call | flops 4000000000 | bytes 4000000 | tf_op jit(solution)/shard_map/far/pallas_call | solution.py:233
Async XLA Ops:
  0.0 16.9 %copy-start = (bf16[1,4,8,48,128]{4,3,2,1,0:T(8,128)(2,1)S(1)}, bf16[1,4,8,48,128]{4,3,2,1,0:T(8,128)(2,1)}, u32[]{:S(2)}) copy-start(bf16[1,4,8,48,128]{4,3,2,1,0:T(8,128)(2,1)} %param.9) | copy-start | bytes 1179652
  1.1 29.3 %collective-permute-start.3 = (bf16[4,2,48,128]{3,2,1,0:T(8,128)(2,1)S(1)}, bf16[4,2,48,128]{3,2,1,0:T(8,128)(2,1)S(1)}, u32[]{:S(2)}, u32[]{:S(2)}) collective-permute-start(bf16[4,2,48,128]{3,2,1,0:T(8,128)(2,1)S(1)} %get-tuple-element.12), channel_id=1, source_target_pairs={{0,18},{2,20},{4,22},{6,24},{8,26},{10,28},{12,30},{16,34},{18,36}... | collective-permute-start | bytes 294920 | tf_op jit(solution)/shard_map/ppermute | solution.py:273
  8.2 12.3 %collective-permute-start = (bf16[4,2,48,128]{3,2,1,0:T(8,128)(2,1)S(1)}, bf16[4,2,48,128]{3,2,1,0:T(8,128)(2,1)S(1)}, u32[]{:S(2)}, u32[]{:S(2)}) collective-permute-start(bf16[4,2,48,128]{3,2,1,0:T(8,128)(2,1)S(1)} %get-tuple-element.12), channel_id=1, source_target_pairs={{0,16},{16,32},{32,48},{48,64},{64,80},{80,96},{96,112},{112,128},... | collective-permute-start | bytes 294920 | tf_op jit(solution)/shard_map/ppermute | solution.py:272
  14.2 16.2 %collective-permute-start.4 = (bf16[4,2,48,128]{3,2,1,0:T(8,128)(2,1)S(1)}, bf16[4,2,48,128]{3,2,1,0:T(8,128)(2,1)S(1)}, u32[]{:S(2)}, u32[]{:S(2)}) collective-permute-start(bf16[4,2,48,128]{3,2,1,0:T(8,128)(2,1)S(1)} %get-tuple-element.13), channel_id=1, source_target_pairs={{16,2},{18,4},{20,6},{22,8},{24,10},{26,12},{28,14},{32,18},{34,20... | collective-permute-start | bytes 294920 | tf_op jit(solution)/shard_map/ppermute | solution.py:271
  15.5 9.4 %collective-permute-start.1 = (bf16[4,2,48,128]{3,2,1,0:T(8,128)(2,1)S(1)}, bf16[4,2,48,128]{3,2,1,0:T(8,128)(2,1)S(1)}, u32[]{:S(2)}, u32[]{:S(2)}) collective-permute-start(bf16[4,2,48,128]{3,2,1,0:T(8,128)(2,1)S(1)} %get-tuple-element.13), channel_id=1, source_target_pairs={{16,0},{32,16},{48,32},{64,48},{80,64},{96,80},{112,96},{128,112},... | collective-permute-start | bytes 294920 | tf_op jit(solution)/shard_map/ppermute | solution.py:274
  16.9 36.3 %collective-permute-start.2 = (bf16[4,8,48,128]{3,2,1,0:T(8,128)(2,1)S(1)}, bf16[4,8,48,128]{3,2,1,0:T(8,128)(2,1)S(1)}, u32[]{:S(2)}, u32[]{:S(2)}) collective-permute-start(bf16[4,8,48,128]{3,2,1,0:T(8,128)(2,1)S(1)} %bitcast.12), channel_id=1, source_target_pairs={{0,2},{2,4},{4,6},{6,8},{8,10},{10,12},{12,14},{1,3},{3,5},{5,7},{... | collective-permute-start | bytes 1179656 | tf_op jit(solution)/shard_map/ppermute | solution.py:269

commit v3 on v2

v3 whole, which is shorter than its diff:
```python
import functools

import jax
import jax.numpy as jnp
from jax import lax
from jax.experimental import pallas as pl
from jax.experimental.pallas import tpu as pltpu
from jax.sharding import PartitionSpec as P


EPS = 1e-06
PAD = 8


def activate(values, gain, shift):
    middle = jnp.mean(values, axis=-1, keepdims=True)
    centred = values - middle
    spread = jnp.mean(centred * centred, axis=-1, keepdims=True)
    half = centred * lax.rsqrt(spread + EPS) * gain + shift
    return half + half * jnp.tanh(half)


def put_shifted(ref, frame, row, slot, values):
    width = values.shape[0]
    slot[PAD : PAD + width] = values
    ref[0, frame, row] = slot[PAD - 1 : PAD - 1 + width].astype(ref.dtype)
    ref[1, frame, row] = values.astype(ref.dtype)
    ref[2, frame, row] = slot[PAD + 1 : PAD + 1 + width].astype(ref.dtype)


def clear_slots(slots):
    for slot in range(slots.shape[0]):
        slots[slot, :PAD] = jnp.zeros((PAD, slots.shape[2]), slots.dtype)
        slots[slot, slots.shape[1] - PAD :] = jnp.zeros((PAD, slots.shape[2]), slots.dtype)


def pair_taps(weight_ref, step_t, step_w):
    top, mid, low = (weight_ref[step_t, i, step_w] for i in range(3))
    none = jnp.zeros_like(top)
    upper = jnp.concatenate([jnp.concatenate([top, none], 1), jnp.concatenate([mid, top], 1)], 0)
    lower = jnp.concatenate([jnp.concatenate([low, mid], 1), jnp.concatenate([none, low], 1)], 0)
    return upper, lower


def conv_pairs(maps_ref, weight_ref, taps, pairs):
    total = None
    for step_t, frame in taps:
        for step_w in range(3):
            for skip, rhs in enumerate(pair_taps(weight_ref, step_t, step_w)):
                rows = [2 * (skip + k) for k in range(pairs)]
                left = jnp.concatenate([maps_ref[step_w, frame, r] for r in rows], 0)
                right = jnp.concatenate([maps_ref[step_w, frame, r + 1] for r in rows], 0)
                lhs = jnp.concatenate([left, right], 1)
                part = jnp.dot(lhs, rhs, preferred_element_type=jnp.float32)
                total = part if total is None else total + part
    return total


def pick(total, row, width, channels):
    pair, half = divmod(row, 2)
    return total[pair * width : (pair + 1) * width, half * channels : (half + 1) * channels]


def ready_kernel(video, top, bottom):
    top[...] = video[:, : top.shape[1]]
    bottom[...] = video[:, video.shape[1] - bottom.shape[1] :]


def masked(values, valid):
    return values if valid is None else jnp.where(valid, values, 0.0)


def own_sums(video, vectors, weights_hbm, table, weights, part1, second, first, slots, sems):
    frames, rows, width, channels = video.shape
    loads = [pltpu.make_async_copy(v, table.at[i], sems.at[i]) for i, v in enumerate(vectors)]
    loads += [pltpu.make_async_copy(h, w, sems.at[6 + i]) for i, (h, w) in enumerate(zip(weights_hbm, weights))]
    for load in loads:
        load.start()
    clear_slots(slots)
    for load in loads[:6]:
        load.wait()
    g1, s1, b1, g2, s2, _ = (table[i] for i in range(6))
    g1, s1, g2, s2 = 0.5 * g1, 0.5 * s1, 0.5 * g2, 0.5 * s2
    half = rows // 2

    def enter(frame):
        for row in range(rows):
            values = activate(video[frame, row].astype(jnp.float32), g1, s1)
            put_shifted(first, frame, row + 2, slots.at[frame * rows + row], values)
        for row in (0, 1, rows + 2, rows + 3):
            for step_w in range(3):
                first[step_w, frame, row] = jnp.zeros((width, channels), first.dtype)

    def middle(total, frame, to):
        part1[frame] = total
        for row in range(2, rows):
            values = activate(pick(total, row, width, channels) + b1, g2, s2)
            put_shifted(second, to, row, slots.at[(frames + to) * rows + row], values)

    enter(0)
    loads[6].wait()
    part1[0] = conv_pairs(first, weights[0], [(2, 0)], half + 1)
    enter(1)
    part1[1] = conv_pairs(first, weights[0], [(1, 0), (2, 1)], half + 1)
    enter(2)
    middle(conv_pairs(first, weights[0], [(0, 0), (1, 1), (2, 2)], half + 1), 2, 0)
    enter(3)
    middle(conv_pairs(first, weights[0], [(0, 1), (1, 2), (2, 3)], half + 1), 3, 1)
    loads[7].wait()


def near_kernel(
    place, video, v0, v1, v2, v3, v4, v5, weight1_hbm, weight2_hbm,
    part1, second, table, weight1, weight2, first, slots, sems,
):
    is_top = jnp.logical_not(place()[1])

    @pl.when(jnp.logical_not(is_top))
    def _():
        own_sums(
            video, (v0, v1, v2, v3, v4, v5), (weight1_hbm, weight2_hbm),
            table, (weight1, weight2), part1, second, first, slots, sems,
        )


def edge_kernel(
    place, video, above, below, v0, v1, v2, v3, v4, v5, weight1_hbm, weight2_hbm, *refs,
):
    part1, second, table, weight1, weight2, part2, first, halo, slots, sems = refs[5:]
    frames, rows, width, channels = video.shape
    _, has_above, has_below = place()

    @pl.when(jnp.logical_not(has_above))
    def _():
        own_sums(
            video, (v0, v1, v2, v3, v4, v5), (weight1_hbm, weight2_hbm),
            table, (weight1, weight2), part1, second, first, slots, sems,
        )

    clear_slots(slots)
    g1, s1, b1, g2, s2, _ = (table[i] for i in range(6))
    g1, s1, g2, s2 = 0.5 * g1, 0.5 * s1, 0.5 * g2, 0.5 * s2
    half = rows // 2
    sides = ((above, has_above, 0, 0), (below, has_below, 1, half))
    for frame in range(frames):
        for ref, valid, side, _ in sides:
            for k in range(2):
                values = masked(activate(ref[frame, k].astype(jnp.float32), g1, s1), valid)
                put_shifted(halo, frame, 2 * side + k, slots.at[4 * frame + 2 * side + k], values)
    sums = {}
    for _, _, side, pair in sides:
        for step_t in range(3):
            count = frames - 2 + step_t
            total = None
            for step_w in range(3):
                rhs = pair_taps(weight1, step_t, step_w)[side]
                left = jnp.concatenate([halo[step_w, f, 2 * side] for f in range(count)], 0)
                right = jnp.concatenate([halo[step_w, f, 2 * side + 1] for f in range(count)], 0)
                part = jnp.dot(jnp.concatenate([left, right], 1), rhs, preferred_element_type=jnp.float32)
                total = part if total is None else total + part
            for f in range(count):
                to = f + 2 - step_t
                part = total[f * width : (f + 1) * width]
                sums[side, to] = part if (side, to) not in sums else sums[side, to] + part
    for to in range(frames):
        for _, valid, side, pair in sides:
            total = part1[to, pair * width : (pair + 1) * width] + sums[side, to]
            if to < 2:
                part1[to, pair * width : (pair + 1) * width] = total
                continue
            for k in range(2):
                row = 2 * pair + k
                values = activate(pick(total, k, width, channels) + b1, g2, s2)
                values = masked(values, valid if row in (0, rows + 1) else None)
                put_shifted(second, to - 2, row, slots.at[4 * (frames + to) + 2 * side + k], values)
    part2[0] = conv_pairs(second, weight2, [(2, 0)], half)
    part2[1] = conv_pairs(second, weight2, [(1, 0), (2, 1)], half)


def far_kernel(
    place, video, above, below, behind, behind_above, behind_below, part1, part2,
    table, weight1, weight2, out, first, second, slots, held, sems,
):
    frames, rows, width, channels = video.shape
    clear_slots(slots)
    is_start, has_above, has_below = place()
    g1, s1, b1, g2, s2, b2 = (table[i] for i in range(6))
    g1, s1, g2, s2 = 0.5 * g1, 0.5 * s1, 0.5 * g2, 0.5 * s2

    def enter(frame):
        for row in range(-2, rows + 2):
            at = row + 2 if row < 0 else row - rows if row >= rows else row
            ref, own = (behind_above, above) if row < 0 else (behind_below, below) if row >= rows else (behind, video)
            values = ref[frame, at]
            if frame >= frames - 2:
                values = jnp.where(is_start, own[0, at], values)
            values = activate(values.astype(jnp.float32), g1, s1)
            values = masked(values, has_above if row < 0 else has_below if row >= rows else None)
            put_shifted(first, frame, row + 2, slots.at[frame * (rows + 4) + row + 2], values)

    def middle(total, to):
        for row in range(rows + 2):
            values = activate(pick(total, row, width, channels) + b1, g2, s2)
            values = masked(values, has_above if row == 0 else has_below if row == rows + 1 else None)
            if to < 2:
                values = jnp.where(is_start, slots[(frames + 2) * (rows + 4) + row, PAD : PAD + width], values)
            put_shifted(second, to, row, slots.at[(frames + to) * (rows + 4) + row], values)

    def leave(total, frame):
        for row in range(rows):
            values = pick(total, row, width, channels) + b2
            held[frame, row] = (video[frame, row].astype(jnp.float32) + values).astype(out.dtype)
        pltpu.make_async_copy(held.at[frame], out.at[frame], sems.at[frame]).start()

    half = rows // 2
    enter(3)
    total = conv_pairs(first, weight1, [(0, 3)], half + 1) + part1[1]
    enter(2)
    middle(total, 3)
    total = conv_pairs(first, weight1, [(0, 2), (1, 3)], half + 1) + part1[0]
    enter(1)
    middle(total, 2)
    total = conv_pairs(first, weight1, [(0, 1), (1, 2), (2, 3)], half + 1)
    enter(0)
    middle(total, 1)
    total = conv_pairs(first, weight1, [(0, 0), (1, 1), (2, 2)], half + 1)
    leave(conv_pairs(second, weight2, [(0, 3)], half) + part2[1], 3)
    leave(conv_pairs(second, weight2, [(0, 2), (1, 3)], half) + part2[0], 2)
    middle(total, 0)
    leave(conv_pairs(second, weight2, [(0, 1), (1, 2), (2, 3)], half), 1)
    leave(conv_pairs(second, weight2, [(0, 0), (1, 1), (2, 2)], half), 0)
    for frame in range(frames):
        pltpu.make_async_copy(held.at[frame], out.at[frame], sems.at[frame]).wait()


VMEM = pl.BlockSpec(memory_space=pltpu.VMEM)
OUTSIDE = pl.BlockSpec(memory_space=pltpu.HBM)
MIB = 1024 * 1024


def hbm(array):
    return pltpu.with_memory_space_constraint(array, pltpu.HBM)


def cost(flops):
    return pl.CostEstimate(flops=flops, bytes_accessed=4 * 10**6, transcendentals=0)


def ready(clip):
    frames, _, width, channels = clip.shape
    edge = jax.ShapeDtypeStruct((frames, 2, width, channels), clip.dtype)
    return pl.pallas_call(
        ready_kernel,
        out_shape=[edge, edge],
        in_specs=[VMEM],
        out_specs=[VMEM] * 2,
        compiler_params=pltpu.CompilerParams(vmem_limit_bytes=4 * MIB),
        name="ready",
    )(clip)


def near(place, clip, vectors, weight1, weight2):
    frames, rows, width, channels = clip.shape
    bf16, f32 = jnp.bfloat16, jnp.float32
    outside = [hbm(v.reshape(1, channels)) for v in vectors] + [hbm(weight1), hbm(weight2)]
    return pl.pallas_call(
        functools.partial(near_kernel, place),
        out_shape=[
            jax.ShapeDtypeStruct((frames, (rows // 2 + 1) * width, 2 * channels), f32),
            jax.ShapeDtypeStruct((3, 2, rows + 2, width, channels), bf16),
            jax.ShapeDtypeStruct((6, 1, channels), f32),
            jax.ShapeDtypeStruct(weight1.shape, bf16),
            jax.ShapeDtypeStruct(weight2.shape, bf16),
        ],
        in_specs=[VMEM] + [OUTSIDE] * 8,
        out_specs=[VMEM] * 5,
        scratch_shapes=[
            pltpu.VMEM((3, frames, rows + 4, width, channels), bf16),
            pltpu.VMEM(((frames + 2) * rows, width + 2 * PAD, channels), f32),
            pltpu.SemaphoreType.DMA((8,)),
        ],
        compiler_params=pltpu.CompilerParams(vmem_limit_bytes=24 * MIB),
        cost_estimate=cost(4 * 10**9),
        name="near",
    )(clip, *outside)


def edge(place, clip, above, below, vectors, weight1, weight2, made):
    frames, rows, width, channels = clip.shape
    bf16, f32 = jnp.bfloat16, jnp.float32
    outside = [hbm(v.reshape(1, channels)) for v in vectors] + [hbm(weight1), hbm(weight2)]
    return pl.pallas_call(
        functools.partial(edge_kernel, place),
        out_shape=[jax.ShapeDtypeStruct(m.shape, m.dtype) for m in made]
        + [jax.ShapeDtypeStruct((2, rows // 2 * width, 2 * channels), f32)],
        in_specs=[VMEM] * 3 + [OUTSIDE] * 8 + [VMEM] * 5,
        out_specs=[VMEM] * 6,
        input_output_aliases={11 + i: i for i in range(5)},
        scratch_shapes=[
            pltpu.VMEM((3, frames, rows + 4, width, channels), bf16),
            pltpu.VMEM((3, frames, 4, width, channels), bf16),
            pltpu.VMEM(((frames + 2) * rows, width + 2 * PAD, channels), f32),
            pltpu.SemaphoreType.DMA((8,)),
        ],
        compiler_params=pltpu.CompilerParams(vmem_limit_bytes=24 * MIB),
        cost_estimate=cost(2 * 10**9),
        name="edge",
    )(clip, above, below, *outside, *made)


def far(place, clip, above, below, behind, behind_above, behind_below, part1, part2, table, weight1, weight2):
    frames, rows, width, channels = clip.shape
    bf16, f32 = jnp.bfloat16, jnp.float32
    return pl.pallas_call(
        functools.partial(far_kernel, place),
        out_shape=jax.ShapeDtypeStruct(clip.shape, clip.dtype),
        in_specs=[VMEM] * 11,
        out_specs=OUTSIDE,
        scratch_shapes=[
            pltpu.VMEM((3, frames, rows + 4, width, channels), bf16),
            pltpu.VMEM((3, frames, rows + 2, width, channels), bf16),
            pltpu.VMEM((2 * frames * (rows + 4), width + 2 * PAD, channels), f32),
            pltpu.VMEM(clip.shape, clip.dtype),
            pltpu.SemaphoreType.DMA((frames,)),
        ],
        compiler_params=pltpu.CompilerParams(vmem_limit_bytes=24 * MIB),
        cost_estimate=cost(4 * 10**9),
        name="far",
    )(clip, above, below, behind, behind_above, behind_below, part1, part2, table, weight1, weight2)


def body(
    video,
    norm1_gain,
    norm1_shift,
    conv1_weight,
    conv1_bias,
    norm2_gain,
    norm2_shift,
    conv2_weight,
    conv2_bias,
):
    clip = video[0]
    spans, slabs = lax.axis_size("ta"), lax.axis_size("ha")
    vectors = (norm1_gain, norm1_shift, conv1_bias, norm2_gain, norm2_shift, conv2_bias)

    def place():
        slab = lax.axis_index("ha")
        return lax.axis_index("ta") == 0, slab > 0, slab < slabs - 1

    def at(h, t):
        return h * spans + t

    up = [(h, h + 1) for h in range(slabs - 1)]
    on = [(t, t + 1) for t in range(spans - 1)]

    behind = lax.ppermute(clip, "ta", on)
    top, bottom = ready(clip)
    behind_below = lax.ppermute(top, ("ha", "ta"), [(at(h, t), at(g, n)) for g, h in up for t, n in on])
    above = lax.ppermute(bottom, "ha", up)
    made = near(place, clip, vectors, conv1_weight, conv2_weight)
    below = lax.ppermute(top, "ha", [(h, g) for g, h in up])
    behind_above = lax.ppermute(bottom, ("ha", "ta"), [(at(g, t), at(h, n)) for g, h in up for t, n in on])
    *made, part2 = edge(place, clip, above, below, vectors, conv1_weight, conv2_weight, made)
    part1, _, table, weight1, weight2 = made
    out = far(
        place, clip, above, below, behind, behind_above, behind_below, part1, part2, table, weight1, weight2
    )
    return out[None]


def solution(mesh):
    placed = (P(("grp", "cam"), "ta", "ha", None, None), P(), P(), P(), P(), P(), P(), P(), P())
    return jax.shard_map(
        body,
        mesh=mesh,
        in_specs=placed,
        out_specs=P(("grp", "cam"), "ta", "ha", None, None),
        check_vma=False,
    )
```

time: 59 us -> 60.5 us (1.025)
  Pallas kernels: 12.1 us -> 14.1 us
    ppermute x1, waiting for transfers between devices: 0.01 us -> 21.9 us  [body(): lax.ppermute(top, ('ha', 'ta'), [(at(h, t), at(g, n)) for g, h in up for...]
    ppermute x1, waiting for transfers between devices: 22.7 us -> 2.91 us  [body(): behind = lax.ppermute(clip, 'ta', on)]
    ppermute x1, waiting for transfers between devices: 4.42 us -> 1.75 us  [body(): below = lax.ppermute(top, 'ha', [(h, g) for g, h in up])]
    pallas_call x3 -> x4, Pallas kernels: 12.1 us -> 14.1 us  [the longest x1 6.31 us: edge(): pl.pallas_call(functools.partial(edge_kernel, place), out_shape=[jax.Shap...]
  transfers between devices with their start and end apart: 5 -> 5, of which waited for: 2 -> 3; matrix products, arithmetic and copies ran while one was open for 0% -> 0% of each run, Pallas kernels for 9% -> 12%
where the time goes in v3:
time: 60.5 us; the launch traced here: 60.1 us
  waiting for transfers between devices  26.6 us (44%)
  starting transfers between devices  19.3 us (32%)
  Pallas kernels  14.1 us (23%)
    ppermute x1, waiting for transfers between devices, body(): lax.ppermute(top, ('ha', 'ta'), [(at(h, t), at(g, n)) for g, h in up for...  21.9 us
    ppermute x1, starting transfers between devices, body(): lax.ppermute(bottom, ('ha', 'ta'), [(at(g, t), at(h, n)) for g, h in up f...  7.09 us
    pallas_call x1, Pallas kernels, edge(): pl.pallas_call(functools.partial(edge_kernel, place), out_shape=[jax.Shap...  6.31 us
    ppermute x1, starting transfers between devices, body(): above = lax.ppermute(bottom, 'ha', up)  6.03 us
    pallas_call x1, Pallas kernels, far(): pl.pallas_call(functools.partial(far_kernel, place), out_shape=jax.ShapeD...  5.73 us
    ppermute x1, starting transfers between devices, body(): behind = lax.ppermute(clip, 'ta', on)  3.57 us
    ppermute x1, waiting for transfers between devices, body(): behind = lax.ppermute(clip, 'ta', on)  2.91 us
    ppermute x1, waiting for transfers between devices, body(): below = lax.ppermute(top, 'ha', [(h, g) for g, h in up])  1.75 us
  transfers between devices with their start and end apart: 5, of which 3 were waited for; matrix products, arithmetic and copies ran while one was open for 0% of the time, Pallas kernels for 12%

profile of v3, /device:TPU:66, one launch (start us, length us, event | category | flops | bytes accessed | tf_op | source)
XLA Modules:
  0.0 60.1 jit_solution(4879618473886630638)
XLA Ops:
  0.0 1.0 %ready.1 = (bf16[4,2,48,128]{3,2,1,0:T(8,128)(2,1)S(1)}, bf16[4,2,48,128]{3,2,1,0:T(8,128)(2,1)S(1)}) custom-call(bf16[4,8,48,128]{3,2,1,0:T(8,128)(2,1)} %bitcast.video), custom_call_target="tpu_custom_call" | custom-call | tf_op jit(solution)/shard_map/ready/pallas_call | solution.py:252
  1.0 6.0 %collective-permute-start = (bf16[4,2,48,128]{3,2,1,0:T(8,128)(2,1)S(1)}, bf16[4,2,48,128]{3,2,1,0:T(8,128)(2,1)S(1)}, u32[]{:S(2)}, u32[]{:S(2)}) collective-permute-start(bf16[4,2,48,128]{3,2,1,0:T(8,128)(2,1)S(1)} %get-tuple-element.17), channel_id=1, source_target_pairs={{0,16},{16,32},{32,48},{48,64},{64,80},{80,96},{96,112},{112,128},... | collective-permute-start | bytes 294920 | tf_op jit(solution)/shard_map/ppermute | solution.py:360
  7.0 7.1 %collective-permute-start.3 = (bf16[4,2,48,128]{3,2,1,0:T(8,128)(2,1)S(1)}, bf16[4,2,48,128]{3,2,1,0:T(8,128)(2,1)S(1)}, u32[]{:S(2)}, u32[]{:S(2)}) collective-permute-start(bf16[4,2,48,128]{3,2,1,0:T(8,128)(2,1)S(1)} %get-tuple-element.17), channel_id=1, source_target_pairs={{0,18},{2,20},{4,22},{6,24},{8,26},{10,28},{12,30},{16,34},{18,36}... | collective-permute-start | bytes 294920 | tf_op jit(solution)/shard_map/ppermute | solution.py:363
  14.2 1.3 %collective-permute-start.1 = (bf16[4,2,48,128]{3,2,1,0:T(8,128)(2,1)S(1)}, bf16[4,2,48,128]{3,2,1,0:T(8,128)(2,1)S(1)}, u32[]{:S(2)}, u32[]{:S(2)}) collective-permute-start(bf16[4,2,48,128]{3,2,1,0:T(8,128)(2,1)S(1)} %get-tuple-element.18), channel_id=1, source_target_pairs={{16,0},{32,16},{48,32},{64,48},{80,64},{96,80},{112,96},{128,112},... | collective-permute-start | bytes 294920 | tf_op jit(solution)/shard_map/ppermute | solution.py:362
  15.5 1.3 %collective-permute-start.4 = (bf16[4,2,48,128]{3,2,1,0:T(8,128)(2,1)S(1)}, bf16[4,2,48,128]{3,2,1,0:T(8,128)(2,1)S(1)}, u32[]{:S(2)}, u32[]{:S(2)}) collective-permute-start(bf16[4,2,48,128]{3,2,1,0:T(8,128)(2,1)S(1)} %get-tuple-element.18), channel_id=1, source_target_pairs={{16,2},{18,4},{20,6},{22,8},{24,10},{26,12},{28,14},{32,18},{34,20... | collective-permute-start | bytes 294920 | tf_op jit(solution)/shard_map/ppermute | solution.py:359
  16.8 3.6 %collective-permute-start.2 = (bf16[4,8,48,128]{3,2,1,0:T(8,128)(2,1)}, bf16[4,8,48,128]{3,2,1,0:T(8,128)(2,1)S(1)}, u32[]{:S(2)}, u32[]{:S(2)}) collective-permute-start(bf16[4,8,48,128]{3,2,1,0:T(8,128)(2,1)} %bitcast.video), channel_id=1, source_target_pairs={{0,2},{2,4},{4,6},{6,8},{8,10},{10,12},{12,14},{1,3},{3,5},{5,7},{... | collective-permute-start | bytes 1179656 | tf_op jit(solution)/shard_map/ppermute | solution.py:357
  20.4 1.1 %near.1 = (f32[4,240,256]{2,1,0:T(8,128)S(1)}, bf16[3,2,10,48,128]{4,3,2,1,0:T(8,128)(2,1)S(1)}, f32[6,1,128]{2,1,0:T(1,128)S(1)}, bf16[3,3,3,128,128]{4,3,2,1,0...) custom-call(bf16[4,8,48,128]{3,2,1,0:T(8,128)(2,1)} %bitcast.video, f32[1,128]{1,0:T(1,128)} %bitcast.8, f32[1,128]{1,0:T(1,128)} %bitcast.10, ...), custom_call_target="tpu_custom_call" | custom-call | flops 4000000000 | bytes 4000000 | tf_op jit(solution)/shard_map/near/pallas_call | solution.py:266
  21.4 0.0 collective-permute-done.above
  21.5 1.8 %collective-permute-done.1.below = bf16[4,2,48,128]{3,2,1,0:T(8,128)(2,1)S(1)} collective-permute-done((bf16[4,2,48,128]{3,2,1,0:T(8,128)(2,1)S(1)}, bf16[4,2,48,128]{3,2,1,0:T(8,128)(2,1)S(1)}, u32[]{:S(2)}, u32[]{:S(2)}) %collective-permute-start.1) | collective-permute-done | bytes 98336 | tf_op jit(solution)/shard_map/ppermute | solution.py:362
  23.2 6.3 %edge.1 = (f32[4,240,256]{2,1,0:T(8,128)S(1)}, bf16[3,2,10,48,128]{4,3,2,1,0:T(8,128)(2,1)S(1)}, f32[6,1,128]{2,1,0:T(1,128)S(1)}, bf16[3,3,3,128,128]{4,3,2,1,0...) custom-call(bf16[4,8,48,128]{3,2,1,0:T(8,128)(2,1)} %bitcast.video, ...), custom_call_target="tpu_custom_call", output_to_operand_aliasing={{0}: (11, {}), {1}: (12, {}), {2}: (13, {}), {3}: (14, {}),... | custom-call | flops 2000000000 | bytes 4000000 | tf_op jit(solution)/shard_map/edge/pallas_call | solution.py:292
  29.5 0.0 collective-permute-done.3.behind_above
  29.5 21.9 %collective-permute-done.4.behind_below = bf16[4,2,48,128]{3,2,1,0:T(8,128)(2,1)S(1)} collective-permute-done((bf16[4,2,48,128]{3,2,1,0:T(8,128)(2,1)S(1)}, bf16[4,2,48,128]{3,2,1,0:T(8,128)(2,1)S(1)}, u32[]{:S(2)}, u32[]{:S(2)}) %collective-permute-start.4) | collective-permute-done | bytes 98336 | tf_op jit(solution)/shard_map/ppermute | solution.py:359
  51.4 2.9 %collective-permute-done.2.behind = bf16[4,8,48,128]{3,2,1,0:T(8,128)(2,1)S(1)} collective-permute-done((bf16[4,8,48,128]{3,2,1,0:T(8,128)(2,1)}, bf16[4,8,48,128]{3,2,1,0:T(8,128)(2,1)S(1)}, u32[]{:S(2)}, u32[]{:S(2)}) %collective-permute-start.2) | collective-permute-done | bytes 393248 | tf_op jit(solution)/shard_map/ppermute | solution.py:357
  54.4 5.7 %far.1 = bf16[4,8,48,128]{3,2,1,0:T(8,128)(2,1)} custom-call(bf16[4,8,48,128]{3,2,1,0:T(8,128)(2,1)} %bitcast.video, bf16[4,2,48,128]{3,2,1,0:T(8,128)(2,1)S(1)} %collective-permute-done.above, bf16[4,2,48,128]{3,2,1,0:T(8,128)(2,1)S(1)} %collective-permute-done.1.below, bf16[4,8,48,128]{3,2,1,0:T(8,128)(2,1)S(1)} %collective-permute-done.2.behind, ...), custom_call_target="tpu_custom_call" | custom-call | flops 4000000000 | bytes 4000000 | tf_op jit(solution)/shard_map/far/pallas_call | solution.py:314
Async XLA Ops:
  1.0 20.4 %collective-permute-start = (bf16[4,2,48,128]{3,2,1,0:T(8,128)(2,1)S(1)}, bf16[4,2,48,128]{3,2,1,0:T(8,128)(2,1)S(1)}, u32[]{:S(2)}, u32[]{:S(2)}) collective-permute-start(bf16[4,2,48,128]{3,2,1,0:T(8,128)(2,1)S(1)} %get-tuple-element.17), channel_id=1, source_target_pairs={{0,16},{16,32},{32,48},{48,64},{64,80},{80,96},{96,112},{112,128},... | collective-permute-start | bytes 294920 | tf_op jit(solution)/shard_map/ppermute | solution.py:360
  7.0 22.5 %collective-permute-start.3 = (bf16[4,2,48,128]{3,2,1,0:T(8,128)(2,1)S(1)}, bf16[4,2,48,128]{3,2,1,0:T(8,128)(2,1)S(1)}, u32[]{:S(2)}, u32[]{:S(2)}) collective-permute-start(bf16[4,2,48,128]{3,2,1,0:T(8,128)(2,1)S(1)} %get-tuple-element.17), channel_id=1, source_target_pairs={{0,18},{2,20},{4,22},{6,24},{8,26},{10,28},{12,30},{16,34},{18,36}... | collective-permute-start | bytes 294920 | tf_op jit(solution)/shard_map/ppermute | solution.py:363
  14.2 9.1 %collective-permute-start.1 = (bf16[4,2,48,128]{3,2,1,0:T(8,128)(2,1)S(1)}, bf16[4,2,48,128]{3,2,1,0:T(8,128)(2,1)S(1)}, u32[]{:S(2)}, u32[]{:S(2)}) collective-permute-start(bf16[4,2,48,128]{3,2,1,0:T(8,128)(2,1)S(1)} %get-tuple-element.18), channel_id=1, source_target_pairs={{16,0},{32,16},{48,32},{64,48},{80,64},{96,80},{112,96},{128,112},... | collective-permute-start | bytes 294920 | tf_op jit(solution)/shard_map/ppermute | solution.py:362
  15.5 36.0 %collective-permute-start.4 = (bf16[4,2,48,128]{3,2,1,0:T(8,128)(2,1)S(1)}, bf16[4,2,48,128]{3,2,1,0:T(8,128)(2,1)S(1)}, u32[]{:S(2)}, u32[]{:S(2)}) collective-permute-start(bf16[4,2,48,128]{3,2,1,0:T(8,128)(2,1)S(1)} %get-tuple-element.18), channel_id=1, source_target_pairs={{16,2},{18,4},{20,6},{22,8},{24,10},{26,12},{28,14},{32,18},{34,20... | collective-permute-start | bytes 294920 | tf_op jit(solution)/shard_map/ppermute | solution.py:359
  16.8 37.6 %collective-permute-start.2 = (bf16[4,8,48,128]{3,2,1,0:T(8,128)(2,1)}, bf16[4,8,48,128]{3,2,1,0:T(8,128)(2,1)S(1)}, u32[]{:S(2)}, u32[]{:S(2)}) collective-permute-start(bf16[4,8,48,128]{3,2,1,0:T(8,128)(2,1)} %bitcast.video), channel_id=1, source_target_pairs={{0,2},{2,4},{4,6},{6,8},{8,10},{10,12},{12,14},{1,3},{3,5},{5,7},{... | collective-permute-start | bytes 1179656 | tf_op jit(solution)/shard_map/ppermute | solution.py:357

commit v4 on v3

--- a/solution.py
+++ b/solution.py
@@ -20,18 +20,23 @@
     return half + half * jnp.tanh(half)
 
 
-def put_shifted(ref, frame, row, slot, values):
+def put_shifted(ref, frame, row, slots, group, values):
     width = values.shape[0]
-    slot[PAD : PAD + width] = values
-    ref[0, frame, row] = slot[PAD - 1 : PAD - 1 + width].astype(ref.dtype)
+    start = row * (width + PAD) + PAD
+    slots[group, start : start + width] = values
+    ref[0, frame, row] = slots[group, start - 1 : start - 1 + width].astype(ref.dtype)
     ref[1, frame, row] = values.astype(ref.dtype)
-    ref[2, frame, row] = slot[PAD + 1 : PAD + 1 + width].astype(ref.dtype)
-
-
-def clear_slots(slots):
-    for slot in range(slots.shape[0]):
-        slots[slot, :PAD] = jnp.zeros((PAD, slots.shape[2]), slots.dtype)
-        slots[slot, slots.shape[1] - PAD :] = jnp.zeros((PAD, slots.shape[2]), slots.dtype)
+    ref[2, frame, row] = slots[group, start + 1 : start + 1 + width].astype(ref.dtype)
+
+
+def slot_shape(groups, rows, width, channels):
+    return groups, rows * (width + PAD) + PAD, channels
+
+
+def clear_slots(slots, width):
+    for group in range(slots.shape[0]):
+        for start in range(0, slots.shape[1], width + PAD):
+            slots[group, start : start + PAD] = jnp.zeros((PAD, slots.shape[2]), slots.dtype)
 
 
 def pair_taps(weight_ref, step_t, step_w):
@@ -71,12 +76,12 @@
 
 
 def own_sums(video, vectors, weights_hbm, table, weights, part1, second, first, slots, sems):
-    frames, rows, width, channels = video.shape
+    _, rows, width, channels = video.shape
     loads = [pltpu.make_async_copy(v, table.at[i], sems.at[i]) for i, v in enumerate(vectors)]
     loads += [pltpu.make_async_copy(h, w, sems.at[6 + i]) for i, (h, w) in enumerate(zip(weights_hbm, weights))]
     for load in loads:
         load.start()
-    clear_slots(slots)
+    clear_slots(slots, width)
     for load in loads[:6]:
         load.wait()
     g1, s1, b1, g2, s2, _ = (table[i] for i in range(6))
@@ -86,7 +91,7 @@
     def enter(frame):
         for row in range(rows):
             values = activate(video[frame, row].astype(jnp.float32), g1, s1)
-            put_shifted(first, frame, row + 2, slots.at[frame * rows + row], values)
+            put_shifted(first, frame, row + 2, slots, frame % 2, values)
         for row in (0, 1, rows + 2, rows + 3):
             for step_w in range(3):
                 first[step_w, frame, row] = jnp.zeros((width, channels), first.dtype)
@@ -95,7 +100,7 @@
         part1[frame] = total
         for row in range(2, rows):
             values = activate(pick(total, row, width, channels) + b1, g2, s2)
-            put_shifted(second, to, row, slots.at[(frames + to) * rows + row], values)
+            put_shifted(second, to, row, slots, 2 + to, values)
 
     enter(0)
     loads[6].wait()
@@ -126,7 +131,7 @@
 def edge_kernel(
     place, video, above, below, v0, v1, v2, v3, v4, v5, weight1_hbm, weight2_hbm, *refs,
 ):
-    part1, second, table, weight1, weight2, part2, first, halo, slots, sems = refs[5:]
+    part1, second, table, weight1, weight2, first, halo, slots, sems = refs[5:]
     frames, rows, width, channels = video.shape
     _, has_above, has_below = place()
 
@@ -137,7 +142,7 @@
             table, (weight1, weight2), part1, second, first, slots, sems,
         )
 
-    clear_slots(slots)
+    clear_slots(slots, width)
     g1, s1, b1, g2, s2, _ = (table[i] for i in range(6))
     g1, s1, g2, s2 = 0.5 * g1, 0.5 * s1, 0.5 * g2, 0.5 * s2
     half = rows // 2
@@ -146,7 +151,7 @@
         for ref, valid, side, _ in sides:
             for k in range(2):
                 values = masked(activate(ref[frame, k].astype(jnp.float32), g1, s1), valid)
-                put_shifted(halo, frame, 2 * side + k, slots.at[4 * frame + 2 * side + k], values)
+                put_shifted(halo, frame, 2 * side + k, slots, frame, values)
     sums = {}
     for _, _, side, pair in sides:
         for step_t in range(3):
@@ -172,63 +177,105 @@
                 row = 2 * pair + k
                 values = activate(pick(total, k, width, channels) + b1, g2, s2)
                 values = masked(values, valid if row in (0, rows + 1) else None)
-                put_shifted(second, to - 2, row, slots.at[4 * (frames + to) + 2 * side + k], values)
-    part2[0] = conv_pairs(second, weight2, [(2, 0)], half)
-    part2[1] = conv_pairs(second, weight2, [(1, 0), (2, 1)], half)
+                put_shifted(second, to - 2, row, slots, to - 2, values)
+
+
+def conv_same(maps_ref, weight_ref, taps, rows):
+    total = None
+    for step_t, frame in taps:
+        for step_w in range(3):
+            top, mid, low = (weight_ref[step_t, i, step_w] for i in range(3))
+            rhs = jnp.concatenate([jnp.concatenate([mid, top], 1), jnp.concatenate([low, mid], 1)], 0)
+            left = jnp.concatenate([maps_ref[step_w, frame, r + 1] for r in rows], 0)
+            right = jnp.concatenate([maps_ref[step_w, frame, r + 2] for r in rows], 0)
+            part = jnp.dot(jnp.concatenate([left, right], 1), rhs, preferred_element_type=jnp.float32)
+            total = part if total is None else total + part
+    return total
+
+
+def conv_next(maps_ref, weight_ref, pairs, rows, step_h):
+    total = None
+    for frames, steps in pairs:
+        for step_w in range(3):
+            none = jnp.zeros(weight_ref.shape[3:], weight_ref.dtype)
+            blocks = [[none if t is None else weight_ref[t, step_h, step_w] for t in line] for line in steps]
+            rhs = jnp.concatenate([jnp.concatenate(line, 1) for line in blocks], 0)
+            sides = [jnp.concatenate([maps_ref[step_w, f, r + 3 * (step_h // 2)] for r in rows], 0) for f in frames]
+            part = jnp.dot(jnp.concatenate(sides, 1), rhs, preferred_element_type=jnp.float32)
+            total = part if total is None else total + part
+    return total
 
 
 def far_kernel(
-    place, video, above, below, behind, behind_above, behind_below, part1, part2,
+    place, video, above, below, behind, behind_above, behind_below, part1, own,
     table, weight1, weight2, out, first, second, slots, held, sems,
 ):
     frames, rows, width, channels = video.shape
-    clear_slots(slots)
     is_start, has_above, has_below = place()
     g1, s1, b1, g2, s2, b2 = (table[i] for i in range(6))
     g1, s1, g2, s2 = 0.5 * g1, 0.5 * s1, 0.5 * g2, 0.5 * s2
+    clear_slots(slots, width)
 
     def enter(frame):
         for row in range(-2, rows + 2):
             at = row + 2 if row < 0 else row - rows if row >= rows else row
-            ref, own = (behind_above, above) if row < 0 else (behind_below, below) if row >= rows else (behind, video)
+            ref, mine = (behind_above, above) if row < 0 else (behind_below, below) if row >= rows else (behind, video)
             values = ref[frame, at]
             if frame >= frames - 2:
-                values = jnp.where(is_start, own[0, at], values)
+                values = jnp.where(is_start, mine[0, at], values)
             values = activate(values.astype(jnp.float32), g1, s1)
             values = masked(values, has_above if row < 0 else has_below if row >= rows else None)
-            put_shifted(first, frame, row + 2, slots.at[frame * (rows + 4) + row + 2], values)
-
-    def middle(total, to):
+            put_shifted(first, frame, row + 2, slots, frame % 2, values)
+
+    def gather(same, sides, which, more, row):
+        pair, half = divmod(row, 2)
+        lines = slice(pair * width, (pair + 1) * width)
+        values = same[lines, half * channels : (half + 1) * channels]
+        values = values + sides[half][lines, which * channels : (which + 1) * channels]
+        return values if more is None else values + more[lines, half * channels : (half + 1) * channels]
+
+    def middle(to, same, sides, which, more, group):
         for row in range(rows + 2):
-            values = activate(pick(total, row, width, channels) + b1, g2, s2)
+            values = activate(gather(same, sides, which, more, row) + b1, g2, s2)
             values = masked(values, has_above if row == 0 else has_below if row == rows + 1 else None)
             if to < 2:
-                values = jnp.where(is_start, slots[(frames + 2) * (rows + 4) + row, PAD : PAD + width], values)
-            put_shifted(second, to, row, slots.at[(frames + to) * (rows + 4) + row], values)
-
-    def leave(total, frame):
+                start = row * (width + PAD) + PAD
+                values = jnp.where(is_start, slots[3, start : start + width], values)
+            put_shifted(second, to, row, slots, group, values)
+
+    def leave(frame, same, sides, which, more):
         for row in range(rows):
-            values = pick(total, row, width, channels) + b2
+            values = gather(same, sides, which, more, row) + b2
             held[frame, row] = (video[frame, row].astype(jnp.float32) + values).astype(out.dtype)
         pltpu.make_async_copy(held.at[frame], out.at[frame], sems.at[frame]).start()
 
     half = rows // 2
+    ins, outs = range(0, rows + 2, 2), range(0, rows, 2)
+    early, late = (((0, 1), ((0, None), (1, 0))), ((2, 3), ((2, 1), (None, 2))))
+    last = ((2, 3), ((0, None), (1, 0)))
+    own3 = conv_pairs(own, weight2, [(1, 0), (2, 1)], half)
+    own2 = conv_pairs(own, weight2, [(2, 0)], half)
     enter(3)
-    total = conv_pairs(first, weight1, [(0, 3)], half + 1) + part1[1]
+    same = conv_same(first, weight1, [(0, 3)], ins)
     enter(2)
-    middle(total, 3)
-    total = conv_pairs(first, weight1, [(0, 2), (1, 3)], half + 1) + part1[0]
+    sides = [conv_next(first, weight1, [last], ins, h) for h in (0, 2)]
+    middle(3, same, sides, 1, part1[1], 2)
+    same = conv_same(first, weight1, [(0, 2), (1, 3)], ins)
     enter(1)
-    middle(total, 2)
-    total = conv_pairs(first, weight1, [(0, 1), (1, 2), (2, 3)], half + 1)
+    middle(2, same, sides, 0, part1[0], 3)
     enter(0)
-    middle(total, 1)
-    total = conv_pairs(first, weight1, [(0, 0), (1, 1), (2, 2)], half + 1)
-    leave(conv_pairs(second, weight2, [(0, 3)], half) + part2[1], 3)
-    leave(conv_pairs(second, weight2, [(0, 2), (1, 3)], half) + part2[0], 2)
-    middle(total, 0)
-    leave(conv_pairs(second, weight2, [(0, 1), (1, 2), (2, 3)], half), 1)
-    leave(conv_pairs(second, weight2, [(0, 0), (1, 1), (2, 2)], half), 0)
+    sides = [conv_next(first, weight1, [late, early], ins, h) for h in (0, 2)]
+    same = conv_same(first, weight1, [(0, 1), (1, 2), (2, 3)], ins)
+    middle(1, same, sides, 1, None, 2)
+    same = conv_same(first, weight1, [(0, 0), (1, 1), (2, 2)], ins)
+    middle(0, same, sides, 0, None, 0)
+    sides = [conv_next(second, weight2, [last], outs, h) for h in (0, 2)]
+    leave(3, conv_same(second, weight2, [(0, 3)], outs), sides, 1, own3)
+    leave(2, conv_same(second, weight2, [(0, 2), (1, 3)], outs), sides, 0, own2)
+    same = conv_same(second, weight2, [(0, 1), (1, 2), (2, 3)], outs)
+    sides = [conv_next(second, weight2, [late, early], outs, h) for h in (0, 2)]
+    leave(1, same, sides, 1, None)
+    leave(0, conv_same(second, weight2, [(0, 0), (1, 1), (2, 2)], outs), sides, 0, None)
     for frame in range(frames):
         pltpu.make_async_copy(held.at[frame], out.at[frame], sems.at[frame]).wait()
 
@@ -276,7 +323,7 @@
         out_specs=[VMEM] * 5,
         scratch_shapes=[
             pltpu.VMEM((3, frames, rows + 4, width, channels), bf16),
-            pltpu.VMEM(((frames + 2) * rows, width + 2 * PAD, channels), f32),
+            pltpu.VMEM(slot_shape(4, rows + 4, width, channels), f32),
             pltpu.SemaphoreType.DMA((8,)),
         ],
         compiler_params=pltpu.CompilerParams(vmem_limit_bytes=24 * MIB),
@@ -291,15 +338,14 @@
     outside = [hbm(v.reshape(1, channels)) for v in vectors] + [hbm(weight1), hbm(weight2)]
     return pl.pallas_call(
         functools.partial(edge_kernel, place),
-        out_shape=[jax.ShapeDtypeStruct(m.shape, m.dtype) for m in made]
-        + [jax.ShapeDtypeStruct((2, rows // 2 * width, 2 * channels), f32)],
+        out_shape=[jax.ShapeDtypeStruct(m.shape, m.dtype) for m in made],
         in_specs=[VMEM] * 3 + [OUTSIDE] * 8 + [VMEM] * 5,
-        out_specs=[VMEM] * 6,
+        out_specs=[VMEM] * 5,
         input_output_aliases={11 + i: i for i in range(5)},
         scratch_shapes=[
             pltpu.VMEM((3, frames, rows + 4, width, channels), bf16),
             pltpu.VMEM((3, frames, 4, width, channels), bf16),
-            pltpu.VMEM(((frames + 2) * rows, width + 2 * PAD, channels), f32),
+            pltpu.VMEM(slot_shape(4, rows + 4, width, channels), f32),
             pltpu.SemaphoreType.DMA((8,)),
         ],
         compiler_params=pltpu.CompilerParams(vmem_limit_bytes=24 * MIB),
@@ -308,7 +354,7 @@
     )(clip, above, below, *outside, *made)
 
 
-def far(place, clip, above, below, behind, behind_above, behind_below, part1, part2, table, weight1, weight2):
+def far(place, clip, above, below, behind, behind_above, behind_below, part1, own, table, weight1, weight2):
     frames, rows, width, channels = clip.shape
     bf16, f32 = jnp.bfloat16, jnp.float32
     return pl.pallas_call(
@@ -319,14 +365,14 @@
         scratch_shapes=[
             pltpu.VMEM((3, frames, rows + 4, width, channels), bf16),
             pltpu.VMEM((3, frames, rows + 2, width, channels), bf16),
-            pltpu.VMEM((2 * frames * (rows + 4), width + 2 * PAD, channels), f32),
+            pltpu.VMEM(slot_shape(4, rows + 4, width, channels), f32),
             pltpu.VMEM(clip.shape, clip.dtype),
             pltpu.SemaphoreType.DMA((frames,)),
         ],
         compiler_params=pltpu.CompilerParams(vmem_limit_bytes=24 * MIB),
         cost_estimate=cost(4 * 10**9),
         name="far",
-    )(clip, above, below, behind, behind_above, behind_below, part1, part2, table, weight1, weight2)
+    )(clip, above, below, behind, behind_above, behind_below, part1, own, table, weight1, weight2)
 
 
 def body(
@@ -357,14 +403,14 @@
     behind = lax.ppermute(clip, "ta", on)
     top, bottom = ready(clip)
     behind_below = lax.ppermute(top, ("ha", "ta"), [(at(h, t), at(g, n)) for g, h in up for t, n in on])
-    above = lax.ppermute(bottom, "ha", up)
     made = near(place, clip, vectors, conv1_weight, conv2_weight)
     below = lax.ppermute(top, "ha", [(h, g) for g, h in up])
+    above = lax.ppermute(bottom, "ha", up)
     behind_above = lax.ppermute(bottom, ("ha", "ta"), [(at(g, t), at(h, n)) for g, h in up for t, n in on])
-    *made, part2 = edge(place, clip, above, below, vectors, conv1_weight, conv2_weight, made)
-    part1, _, table, weight1, weight2 = made
+    made = edge(place, clip, above, below, vectors, conv1_weight, conv2_weight, made)
+    part1, own, table, weight1, weight2 = made
     out = far(
-        place, clip, above, below, behind, behind_above, behind_below, part1, part2, table, weight1, weight2
+        place, clip, above, below, behind, behind_above, behind_below, part1, own, table, weight1, weight2
     )
     return out[None]
 

time: 60.5 us -> 60.2 us (level)
  Pallas kernels: 14.1 us -> 13 us
  waiting for transfers between devices: 26.6 us -> 27.4 us
    ppermute x1, waiting for transfers between devices: 21.9 us -> 22.7 us  [body(): lax.ppermute(top, ('ha', 'ta'), [(at(h, t), at(g, n)) for g, h in up for...]
    pallas_call x1, Pallas kernels: 6.31 us -> 5.52 us  [edge(): pl.pallas_call(functools.partial(edge_kernel, place), out_shape=[jax.Shap...]
  transfers between devices with their start and end apart: 5 -> 5, of which waited for: 3 -> 3; matrix products, arithmetic and copies ran while one was open for 0% -> 0% of each run, Pallas kernels for 12% -> 11%
where the time goes in v4:
time: 60.2 us; the launch traced here: 59.8 us
  waiting for transfers between devices  27.4 us (46%)
  starting transfers between devices  19.3 us (32%)
  Pallas kernels  13 us (22%)
    ppermute x1, waiting for transfers between devices, body(): lax.ppermute(top, ('ha', 'ta'), [(at(h, t), at(g, n)) for g, h in up for...  22.7 us
    ppermute x1, starting transfers between devices, body(): lax.ppermute(bottom, ('ha', 'ta'), [(at(g, t), at(h, n)) for g, h in up f...  7.09 us
    ppermute x1, starting transfers between devices, body(): above = lax.ppermute(bottom, 'ha', up)  6.03 us
    pallas_call x1, Pallas kernels, edge(): pl.pallas_call(functools.partial(edge_kernel, place), out_shape=[jax.Shap...  5.52 us
    pallas_call x1, Pallas kernels, far(): pl.pallas_call(functools.partial(far_kernel, place), out_shape=jax.ShapeD...  5.43 us
    ppermute x1, starting transfers between devices, body(): behind = lax.ppermute(clip, 'ta', on)  3.57 us
    ppermute x1, waiting for transfers between devices, body(): behind = lax.ppermute(clip, 'ta', on)  2.91 us
    ppermute x1, waiting for transfers between devices, body(): below = lax.ppermute(top, 'ha', [(h, g) for g, h in up])  1.75 us
  transfers between devices with their start and end apart: 5, of which 3 were waited for; matrix products, arithmetic and copies ran while one was open for 0% of the time, Pallas kernels for 11%

profile of v4, /device:TPU:66, one launch (start us, length us, event | category | flops | bytes accessed | tf_op | source)
XLA Modules:
  0.0 59.8 jit_solution(9302478851596047272)
XLA Ops:
  0.0 1.0 %ready.1 = (bf16[4,2,48,128]{3,2,1,0:T(8,128)(2,1)S(1)}, bf16[4,2,48,128]{3,2,1,0:T(8,128)(2,1)S(1)}) custom-call(bf16[4,8,48,128]{3,2,1,0:T(8,128)(2,1)} %bitcast.video), custom_call_target="tpu_custom_call" | custom-call | tf_op jit(solution)/shard_map/ready/pallas_call | solution.py:299
  1.0 6.0 %collective-permute-start = (bf16[4,2,48,128]{3,2,1,0:T(8,128)(2,1)S(1)}, bf16[4,2,48,128]{3,2,1,0:T(8,128)(2,1)S(1)}, u32[]{:S(2)}, u32[]{:S(2)}) collective-permute-start(bf16[4,2,48,128]{3,2,1,0:T(8,128)(2,1)S(1)} %get-tuple-element.17), channel_id=1, source_target_pairs={{0,16},{16,32},{32,48},{48,64},{64,80},{80,96},{96,112},{112,128},... | collective-permute-start | bytes 294920 | tf_op jit(solution)/shard_map/ppermute | solution.py:408
  7.0 7.1 %collective-permute-start.3 = (bf16[4,2,48,128]{3,2,1,0:T(8,128)(2,1)S(1)}, bf16[4,2,48,128]{3,2,1,0:T(8,128)(2,1)S(1)}, u32[]{:S(2)}, u32[]{:S(2)}) collective-permute-start(bf16[4,2,48,128]{3,2,1,0:T(8,128)(2,1)S(1)} %get-tuple-element.17), channel_id=1, source_target_pairs={{0,18},{2,20},{4,22},{6,24},{8,26},{10,28},{12,30},{16,34},{18,36}... | collective-permute-start | bytes 294920 | tf_op jit(solution)/shard_map/ppermute | solution.py:409
  14.2 1.3 %collective-permute-start.1 = (bf16[4,2,48,128]{3,2,1,0:T(8,128)(2,1)S(1)}, bf16[4,2,48,128]{3,2,1,0:T(8,128)(2,1)S(1)}, u32[]{:S(2)}, u32[]{:S(2)}) collective-permute-start(bf16[4,2,48,128]{3,2,1,0:T(8,128)(2,1)S(1)} %get-tuple-element.18), channel_id=1, source_target_pairs={{16,0},{32,16},{48,32},{64,48},{80,64},{96,80},{112,96},{128,112},... | collective-permute-start | bytes 294920 | tf_op jit(solution)/shard_map/ppermute | solution.py:407
  15.5 1.3 %collective-permute-start.4 = (bf16[4,2,48,128]{3,2,1,0:T(8,128)(2,1)S(1)}, bf16[4,2,48,128]{3,2,1,0:T(8,128)(2,1)S(1)}, u32[]{:S(2)}, u32[]{:S(2)}) collective-permute-start(bf16[4,2,48,128]{3,2,1,0:T(8,128)(2,1)S(1)} %get-tuple-element.18), channel_id=1, source_target_pairs={{16,2},{18,4},{20,6},{22,8},{24,10},{26,12},{28,14},{32,18},{34,20... | collective-permute-start | bytes 294920 | tf_op jit(solution)/shard_map/ppermute | solution.py:405
  16.8 3.6 %collective-permute-start.2 = (bf16[4,8,48,128]{3,2,1,0:T(8,128)(2,1)}, bf16[4,8,48,128]{3,2,1,0:T(8,128)(2,1)S(1)}, u32[]{:S(2)}, u32[]{:S(2)}) collective-permute-start(bf16[4,8,48,128]{3,2,1,0:T(8,128)(2,1)} %bitcast.video), channel_id=1, source_target_pairs={{0,2},{2,4},{4,6},{6,8},{8,10},{10,12},{12,14},{1,3},{3,5},{5,7},{... | collective-permute-start | bytes 1179656 | tf_op jit(solution)/shard_map/ppermute | solution.py:403
  20.4 1.1 %near.1 = (f32[4,240,256]{2,1,0:T(8,128)S(1)}, bf16[3,2,10,48,128]{4,3,2,1,0:T(8,128)(2,1)S(1)}, f32[6,1,128]{2,1,0:T(1,128)S(1)}, bf16[3,3,3,128,128]{4,3,2,1,0...) custom-call(bf16[4,8,48,128]{3,2,1,0:T(8,128)(2,1)} %bitcast.video, f32[1,128]{1,0:T(1,128)} %bitcast.8, f32[1,128]{1,0:T(1,128)} %bitcast.10, ...), custom_call_target="tpu_custom_call" | custom-call | flops 4000000000 | bytes 4000000 | tf_op jit(solution)/shard_map/near/pallas_call | solution.py:313
  21.4 0.0 collective-permute-done.above
  21.5 1.8 %collective-permute-done.1.below = bf16[4,2,48,128]{3,2,1,0:T(8,128)(2,1)S(1)} collective-permute-done((bf16[4,2,48,128]{3,2,1,0:T(8,128)(2,1)S(1)}, bf16[4,2,48,128]{3,2,1,0:T(8,128)(2,1)S(1)}, u32[]{:S(2)}, u32[]{:S(2)}) %collective-permute-start.1) | collective-permute-done | bytes 98336 | tf_op jit(solution)/shard_map/ppermute | solution.py:407
  23.2 5.5 %edge.1 = (f32[4,240,256]{2,1,0:T(8,128)S(1)}, bf16[3,2,10,48,128]{4,3,2,1,0:T(8,128)(2,1)S(1)}, f32[6,1,128]{2,1,0:T(1,128)S(1)}, bf16[3,3,3,128,128]{4,3,2,1,0...) custom-call(bf16[4,8,48,128]{3,2,1,0:T(8,128)(2,1)} %bitcast.video, ...), custom_call_target="tpu_custom_call", output_to_operand_aliasing={{0}: (11, {}), {1}: (12, {}), {2}: (13, {}), {3}: (14, {}),... | custom-call | flops 2000000000 | bytes 4000000 | tf_op jit(solution)/shard_map/edge/pallas_call | solution.py:339
  28.7 0.0 collective-permute-done.3.behind_above
  28.7 22.7 %collective-permute-done.4.behind_below = bf16[4,2,48,128]{3,2,1,0:T(8,128)(2,1)S(1)} collective-permute-done((bf16[4,2,48,128]{3,2,1,0:T(8,128)(2,1)S(1)}, bf16[4,2,48,128]{3,2,1,0:T(8,128)(2,1)S(1)}, u32[]{:S(2)}, u32[]{:S(2)}) %collective-permute-start.4) | collective-permute-done | bytes 98336 | tf_op jit(solution)/shard_map/ppermute | solution.py:405
  51.4 2.9 %collective-permute-done.2.behind = bf16[4,8,48,128]{3,2,1,0:T(8,128)(2,1)S(1)} collective-permute-done((bf16[4,8,48,128]{3,2,1,0:T(8,128)(2,1)}, bf16[4,8,48,128]{3,2,1,0:T(8,128)(2,1)S(1)}, u32[]{:S(2)}, u32[]{:S(2)}) %collective-permute-start.2) | collective-permute-done | bytes 393248 | tf_op jit(solution)/shard_map/ppermute | solution.py:403
  54.4 5.4 %far.1 = bf16[4,8,48,128]{3,2,1,0:T(8,128)(2,1)} custom-call(bf16[4,8,48,128]{3,2,1,0:T(8,128)(2,1)} %bitcast.video, bf16[4,2,48,128]{3,2,1,0:T(8,128)(2,1)S(1)} %collective-permute-done.above, bf16[4,2,48,128]{3,2,1,0:T(8,128)(2,1)S(1)} %collective-permute-done.1.below, bf16[4,8,48,128]{3,2,1,0:T(8,128)(2,1)S(1)} %collective-permute-done.2.behind, ...), custom_call_target="tpu_custom_call" | custom-call | flops 4000000000 | bytes 4000000 | tf_op jit(solution)/shard_map/far/pallas_call | solution.py:360
Async XLA Ops:
  1.0 20.4 %collective-permute-start = (bf16[4,2,48,128]{3,2,1,0:T(8,128)(2,1)S(1)}, bf16[4,2,48,128]{3,2,1,0:T(8,128)(2,1)S(1)}, u32[]{:S(2)}, u32[]{:S(2)}) collective-permute-start(bf16[4,2,48,128]{3,2,1,0:T(8,128)(2,1)S(1)} %get-tuple-element.17), channel_id=1, source_target_pairs={{0,16},{16,32},{32,48},{48,64},{64,80},{80,96},{96,112},{112,128},... | collective-permute-start | bytes 294920 | tf_op jit(solution)/shard_map/ppermute | solution.py:408
  7.0 21.7 %collective-permute-start.3 = (bf16[4,2,48,128]{3,2,1,0:T(8,128)(2,1)S(1)}, bf16[4,2,48,128]{3,2,1,0:T(8,128)(2,1)S(1)}, u32[]{:S(2)}, u32[]{:S(2)}) collective-permute-start(bf16[4,2,48,128]{3,2,1,0:T(8,128)(2,1)S(1)} %get-tuple-element.17), channel_id=1, source_target_pairs={{0,18},{2,20},{4,22},{6,24},{8,26},{10,28},{12,30},{16,34},{18,36}... | collective-permute-start | bytes 294920 | tf_op jit(solution)/shard_map/ppermute | solution.py:409
  14.2 9.1 %collective-permute-start.1 = (bf16[4,2,48,128]{3,2,1,0:T(8,128)(2,1)S(1)}, bf16[4,2,48,128]{3,2,1,0:T(8,128)(2,1)S(1)}, u32[]{:S(2)}, u32[]{:S(2)}) collective-permute-start(bf16[4,2,48,128]{3,2,1,0:T(8,128)(2,1)S(1)} %get-tuple-element.18), channel_id=1, source_target_pairs={{16,0},{32,16},{48,32},{64,48},{80,64},{96,80},{112,96},{128,112},... | collective-permute-start | bytes 294920 | tf_op jit(solution)/shard_map/ppermute | solution.py:407
  15.5 36.0 %collective-permute-start.4 = (bf16[4,2,48,128]{3,2,1,0:T(8,128)(2,1)S(1)}, bf16[4,2,48,128]{3,2,1,0:T(8,128)(2,1)S(1)}, u32[]{:S(2)}, u32[]{:S(2)}) collective-permute-start(bf16[4,2,48,128]{3,2,1,0:T(8,128)(2,1)S(1)} %get-tuple-element.18), channel_id=1, source_target_pairs={{16,2},{18,4},{20,6},{22,8},{24,10},{26,12},{28,14},{32,18},{34,20... | collective-permute-start | bytes 294920 | tf_op jit(solution)/shard_map/ppermute | solution.py:405
  16.8 37.6 %collective-permute-start.2 = (bf16[4,8,48,128]{3,2,1,0:T(8,128)(2,1)}, bf16[4,8,48,128]{3,2,1,0:T(8,128)(2,1)S(1)}, u32[]{:S(2)}, u32[]{:S(2)}) collective-permute-start(bf16[4,8,48,128]{3,2,1,0:T(8,128)(2,1)} %bitcast.video), channel_id=1, source_target_pairs={{0,2},{2,4},{4,6},{6,8},{8,10},{10,12},{12,14},{1,3},{3,5},{5,7},{... | collective-permute-start | bytes 1179656 | tf_op jit(solution)/shard_map/ppermute | solution.py:403

commit v5 on v4

--- a/solution.py
+++ b/solution.py
@@ -227,16 +227,18 @@
             values = masked(values, has_above if row < 0 else has_below if row >= rows else None)
             put_shifted(first, frame, row + 2, slots, frame % 2, values)
 
-    def gather(same, sides, which, more, row):
+    def gather(same, sides, which, row):
         pair, half = divmod(row, 2)
         lines = slice(pair * width, (pair + 1) * width)
         values = same[lines, half * channels : (half + 1) * channels]
-        values = values + sides[half][lines, which * channels : (which + 1) * channels]
-        return values if more is None else values + more[lines, half * channels : (half + 1) * channels]
+        return values + sides[half][lines, which * channels : (which + 1) * channels]
 
     def middle(to, same, sides, which, more, group):
         for row in range(rows + 2):
-            values = activate(gather(same, sides, which, more, row) + b1, g2, s2)
+            values = gather(same, sides, which, row)
+            if more is not None:
+                values = values + pick(more, row, width, channels)
+            values = activate(values + b1, g2, s2)
             values = masked(values, has_above if row == 0 else has_below if row == rows + 1 else None)
             if to < 2:
                 start = row * (width + PAD) + PAD
@@ -245,16 +247,18 @@
 
     def leave(frame, same, sides, which, more):
         for row in range(rows):
-            values = gather(same, sides, which, more, row) + b2
+            values = gather(same, sides, which, row) + b2
+            if more is not None:
+                values = values + gather(more, own_sides, which, row)
             held[frame, row] = (video[frame, row].astype(jnp.float32) + values).astype(out.dtype)
         pltpu.make_async_copy(held.at[frame], out.at[frame], sems.at[frame]).start()
 
-    half = rows // 2
     ins, outs = range(0, rows + 2, 2), range(0, rows, 2)
     early, late = (((0, 1), ((0, None), (1, 0))), ((2, 3), ((2, 1), (None, 2))))
     last = ((2, 3), ((0, None), (1, 0)))
-    own3 = conv_pairs(own, weight2, [(1, 0), (2, 1)], half)
-    own2 = conv_pairs(own, weight2, [(2, 0)], half)
+    own3 = conv_same(own, weight2, [(1, 0), (2, 1)], outs)
+    own2 = conv_same(own, weight2, [(2, 0)], outs)
+    own_sides = [conv_next(own, weight2, [((0, 1), ((2, 1), (None, 2)))], outs, h) for h in (0, 2)]
     enter(3)
     same = conv_same(first, weight1, [(0, 3)], ins)
     enter(2)
@@ -403,9 +407,9 @@
     behind = lax.ppermute(clip, "ta", on)
     top, bottom = ready(clip)
     behind_below = lax.ppermute(top, ("ha", "ta"), [(at(h, t), at(g, n)) for g, h in up for t, n in on])
+    above = lax.ppermute(bottom, "ha", up)
     made = near(place, clip, vectors, conv1_weight, conv2_weight)
     below = lax.ppermute(top, "ha", [(h, g) for g, h in up])
-    above = lax.ppermute(bottom, "ha", up)
     behind_above = lax.ppermute(bottom, ("ha", "ta"), [(at(g, t), at(h, n)) for g, h in up for t, n in on])
     made = edge(place, clip, above, below, vectors, conv1_weight, conv2_weight, made)
     part1, own, table, weight1, weight2 = made

time: 60.2 us -> 59.9 us (level)
  no operation moved by 1% of the time
where the time goes in v5:
time: 59.9 us; the launch traced here: 59.5 us
  waiting for transfers between devices  27.4 us (46%)
  starting transfers between devices  19.3 us (32%)
  Pallas kernels  12.8 us (21%)
    ppermute x1, waiting for transfers between devices, body(): lax.ppermute(top, ('ha', 'ta'), [(at(h, t), at(g, n)) for g, h in up for...  22.7 us
    ppermute x1, starting transfers between devices, body(): lax.ppermute(bottom, ('ha', 'ta'), [(at(g, t), at(h, n)) for g, h in up f...  7.09 us
    ppermute x1, starting transfers between devices, body(): above = lax.ppermute(bottom, 'ha', up)  6.03 us
    pallas_call x1, Pallas kernels, edge(): pl.pallas_call(functools.partial(edge_kernel, place), out_shape=[jax.Shap...  5.52 us
    pallas_call x1, Pallas kernels, far(): pl.pallas_call(functools.partial(far_kernel, place), out_shape=jax.ShapeD...  5.19 us
    ppermute x1, starting transfers between devices, body(): behind = lax.ppermute(clip, 'ta', on)  3.57 us
    ppermute x1, waiting for transfers between devices, body(): behind = lax.ppermute(clip, 'ta', on)  2.91 us
    ppermute x1, waiting for transfers between devices, body(): below = lax.ppermute(top, 'ha', [(h, g) for g, h in up])  1.75 us
  transfers between devices with their start and end apart: 5, of which 3 were waited for; matrix products, arithmetic and copies ran while one was open for 0% of the time, Pallas kernels for 11%

profile of v5, /device:TPU:66, one launch (start us, length us, event | category | flops | bytes accessed | tf_op | source)
XLA Modules:
  0.0 59.5 jit_solution(2070130953887013625)
XLA Ops:
  0.0 1.0 %ready.1 = (bf16[4,2,48,128]{3,2,1,0:T(8,128)(2,1)S(1)}, bf16[4,2,48,128]{3,2,1,0:T(8,128)(2,1)S(1)}) custom-call(bf16[4,8,48,128]{3,2,1,0:T(8,128)(2,1)} %bitcast.video), custom_call_target="tpu_custom_call" | custom-call | tf_op jit(solution)/shard_map/ready/pallas_call | solution.py:303
  1.0 6.0 %collective-permute-start = (bf16[4,2,48,128]{3,2,1,0:T(8,128)(2,1)S(1)}, bf16[4,2,48,128]{3,2,1,0:T(8,128)(2,1)S(1)}, u32[]{:S(2)}, u32[]{:S(2)}) collective-permute-start(bf16[4,2,48,128]{3,2,1,0:T(8,128)(2,1)S(1)} %get-tuple-element.17), channel_id=1, source_target_pairs={{0,16},{16,32},{32,48},{48,64},{64,80},{80,96},{96,112},{112,128},... | collective-permute-start | bytes 294920 | tf_op jit(solution)/shard_map/ppermute | solution.py:410
  7.0 7.1 %collective-permute-start.3 = (bf16[4,2,48,128]{3,2,1,0:T(8,128)(2,1)S(1)}, bf16[4,2,48,128]{3,2,1,0:T(8,128)(2,1)S(1)}, u32[]{:S(2)}, u32[]{:S(2)}) collective-permute-start(bf16[4,2,48,128]{3,2,1,0:T(8,128)(2,1)S(1)} %get-tuple-element.17), channel_id=1, source_target_pairs={{0,18},{2,20},{4,22},{6,24},{8,26},{10,28},{12,30},{16,34},{18,36}... | collective-permute-start | bytes 294920 | tf_op jit(solution)/shard_map/ppermute | solution.py:413
  14.2 1.3 %collective-permute-start.1 = (bf16[4,2,48,128]{3,2,1,0:T(8,128)(2,1)S(1)}, bf16[4,2,48,128]{3,2,1,0:T(8,128)(2,1)S(1)}, u32[]{:S(2)}, u32[]{:S(2)}) collective-permute-start(bf16[4,2,48,128]{3,2,1,0:T(8,128)(2,1)S(1)} %get-tuple-element.18), channel_id=1, source_target_pairs={{16,0},{32,16},{48,32},{64,48},{80,64},{96,80},{112,96},{128,112},... | collective-permute-start | bytes 294920 | tf_op jit(solution)/shard_map/ppermute | solution.py:412
  15.5 1.3 %collective-permute-start.4 = (bf16[4,2,48,128]{3,2,1,0:T(8,128)(2,1)S(1)}, bf16[4,2,48,128]{3,2,1,0:T(8,128)(2,1)S(1)}, u32[]{:S(2)}, u32[]{:S(2)}) collective-permute-start(bf16[4,2,48,128]{3,2,1,0:T(8,128)(2,1)S(1)} %get-tuple-element.18), channel_id=1, source_target_pairs={{16,2},{18,4},{20,6},{22,8},{24,10},{26,12},{28,14},{32,18},{34,20... | collective-permute-start | bytes 294920 | tf_op jit(solution)/shard_map/ppermute | solution.py:409
  16.8 3.6 %collective-permute-start.2 = (bf16[4,8,48,128]{3,2,1,0:T(8,128)(2,1)}, bf16[4,8,48,128]{3,2,1,0:T(8,128)(2,1)S(1)}, u32[]{:S(2)}, u32[]{:S(2)}) collective-permute-start(bf16[4,8,48,128]{3,2,1,0:T(8,128)(2,1)} %bitcast.video), channel_id=1, source_target_pairs={{0,2},{2,4},{4,6},{6,8},{8,10},{10,12},{12,14},{1,3},{3,5},{5,7},{... | collective-permute-start | bytes 1179656 | tf_op jit(solution)/shard_map/ppermute | solution.py:407
  20.4 1.1 %near.1 = (f32[4,240,256]{2,1,0:T(8,128)S(1)}, bf16[3,2,10,48,128]{4,3,2,1,0:T(8,128)(2,1)S(1)}, f32[6,1,128]{2,1,0:T(1,128)S(1)}, bf16[3,3,3,128,128]{4,3,2,1,0...) custom-call(bf16[4,8,48,128]{3,2,1,0:T(8,128)(2,1)} %bitcast.video, f32[1,128]{1,0:T(1,128)} %bitcast.8, f32[1,128]{1,0:T(1,128)} %bitcast.10, ...), custom_call_target="tpu_custom_call" | custom-call | flops 4000000000 | bytes 4000000 | tf_op jit(solution)/shard_map/near/pallas_call | solution.py:317
  21.4 0.0 collective-permute-done.above
  21.5 1.8 %collective-permute-done.1.below = bf16[4,2,48,128]{3,2,1,0:T(8,128)(2,1)S(1)} collective-permute-done((bf16[4,2,48,128]{3,2,1,0:T(8,128)(2,1)S(1)}, bf16[4,2,48,128]{3,2,1,0:T(8,128)(2,1)S(1)}, u32[]{:S(2)}, u32[]{:S(2)}) %collective-permute-start.1) | collective-permute-done | bytes 98336 | tf_op jit(solution)/shard_map/ppermute | solution.py:412
  23.2 5.5 %edge.1 = (f32[4,240,256]{2,1,0:T(8,128)S(1)}, bf16[3,2,10,48,128]{4,3,2,1,0:T(8,128)(2,1)S(1)}, f32[6,1,128]{2,1,0:T(1,128)S(1)}, bf16[3,3,3,128,128]{4,3,2,1,0...) custom-call(bf16[4,8,48,128]{3,2,1,0:T(8,128)(2,1)} %bitcast.video, ...), custom_call_target="tpu_custom_call", output_to_operand_aliasing={{0}: (11, {}), {1}: (12, {}), {2}: (13, {}), {3}: (14, {}),... | custom-call | flops 2000000000 | bytes 4000000 | tf_op jit(solution)/shard_map/edge/pallas_call | solution.py:343
  28.7 0.0 collective-permute-done.3.behind_above
  28.7 22.7 %collective-permute-done.4.behind_below = bf16[4,2,48,128]{3,2,1,0:T(8,128)(2,1)S(1)} collective-permute-done((bf16[4,2,48,128]{3,2,1,0:T(8,128)(2,1)S(1)}, bf16[4,2,48,128]{3,2,1,0:T(8,128)(2,1)S(1)}, u32[]{:S(2)}, u32[]{:S(2)}) %collective-permute-start.4) | collective-permute-done | bytes 98336 | tf_op jit(solution)/shard_map/ppermute | solution.py:409
  51.4 2.9 %collective-permute-done.2.behind = bf16[4,8,48,128]{3,2,1,0:T(8,128)(2,1)S(1)} collective-permute-done((bf16[4,8,48,128]{3,2,1,0:T(8,128)(2,1)}, bf16[4,8,48,128]{3,2,1,0:T(8,128)(2,1)S(1)}, u32[]{:S(2)}, u32[]{:S(2)}) %collective-permute-start.2) | collective-permute-done | bytes 393248 | tf_op jit(solution)/shard_map/ppermute | solution.py:407
  54.4 5.2 %far.1 = bf16[4,8,48,128]{3,2,1,0:T(8,128)(2,1)} custom-call(bf16[4,8,48,128]{3,2,1,0:T(8,128)(2,1)} %bitcast.video, bf16[4,2,48,128]{3,2,1,0:T(8,128)(2,1)S(1)} %collective-permute-done.above, bf16[4,2,48,128]{3,2,1,0:T(8,128)(2,1)S(1)} %collective-permute-done.1.below, bf16[4,8,48,128]{3,2,1,0:T(8,128)(2,1)S(1)} %collective-permute-done.2.behind, ...), custom_call_target="tpu_custom_call" | custom-call | flops 4000000000 | bytes 4000000 | tf_op jit(solution)/shard_map/far/pallas_call | solution.py:364
Async XLA Ops:
  1.0 20.4 %collective-permute-start = (bf16[4,2,48,128]{3,2,1,0:T(8,128)(2,1)S(1)}, bf16[4,2,48,128]{3,2,1,0:T(8,128)(2,1)S(1)}, u32[]{:S(2)}, u32[]{:S(2)}) collective-permute-start(bf16[4,2,48,128]{3,2,1,0:T(8,128)(2,1)S(1)} %get-tuple-element.17), channel_id=1, source_target_pairs={{0,16},{16,32},{32,48},{48,64},{64,80},{80,96},{96,112},{112,128},... | collective-permute-start | bytes 294920 | tf_op jit(solution)/shard_map/ppermute | solution.py:410
  7.0 21.7 %collective-permute-start.3 = (bf16[4,2,48,128]{3,2,1,0:T(8,128)(2,1)S(1)}, bf16[4,2,48,128]{3,2,1,0:T(8,128)(2,1)S(1)}, u32[]{:S(2)}, u32[]{:S(2)}) collective-permute-start(bf16[4,2,48,128]{3,2,1,0:T(8,128)(2,1)S(1)} %get-tuple-element.17), channel_id=1, source_target_pairs={{0,18},{2,20},{4,22},{6,24},{8,26},{10,28},{12,30},{16,34},{18,36}... | collective-permute-start | bytes 294920 | tf_op jit(solution)/shard_map/ppermute | solution.py:413
  14.2 9.1 %collective-permute-start.1 = (bf16[4,2,48,128]{3,2,1,0:T(8,128)(2,1)S(1)}, bf16[4,2,48,128]{3,2,1,0:T(8,128)(2,1)S(1)}, u32[]{:S(2)}, u32[]{:S(2)}) collective-permute-start(bf16[4,2,48,128]{3,2,1,0:T(8,128)(2,1)S(1)} %get-tuple-element.18), channel_id=1, source_target_pairs={{16,0},{32,16},{48,32},{64,48},{80,64},{96,80},{112,96},{128,112},... | collective-permute-start | bytes 294920 | tf_op jit(solution)/shard_map/ppermute | solution.py:412
  15.5 36.0 %collective-permute-start.4 = (bf16[4,2,48,128]{3,2,1,0:T(8,128)(2,1)S(1)}, bf16[4,2,48,128]{3,2,1,0:T(8,128)(2,1)S(1)}, u32[]{:S(2)}, u32[]{:S(2)}) collective-permute-start(bf16[4,2,48,128]{3,2,1,0:T(8,128)(2,1)S(1)} %get-tuple-element.18), channel_id=1, source_target_pairs={{16,2},{18,4},{20,6},{22,8},{24,10},{26,12},{28,14},{32,18},{34,20... | collective-permute-start | bytes 294920 | tf_op jit(solution)/shard_map/ppermute | solution.py:409
  16.8 37.6 %collective-permute-start.2 = (bf16[4,8,48,128]{3,2,1,0:T(8,128)(2,1)}, bf16[4,8,48,128]{3,2,1,0:T(8,128)(2,1)S(1)}, u32[]{:S(2)}, u32[]{:S(2)}) collective-permute-start(bf16[4,8,48,128]{3,2,1,0:T(8,128)(2,1)} %bitcast.video), channel_id=1, source_target_pairs={{0,2},{2,4},{4,6},{6,8},{8,10},{10,12},{12,14},{1,3},{3,5},{5,7},{... | collective-permute-start | bytes 1179656 | tf_op jit(solution)/shard_map/ppermute | solution.py:407

commit v6 on v5

--- a/solution.py
+++ b/solution.py
@@ -66,9 +66,15 @@
     return total[pair * width : (pair + 1) * width, half * channels : (half + 1) * channels]
 
 
-def ready_kernel(video, top, bottom):
-    top[...] = video[:, : top.shape[1]]
-    bottom[...] = video[:, video.shape[1] - bottom.shape[1] :]
+def ready_kernel(video, top, bottom, sems):
+    loads = [
+        pltpu.make_async_copy(video.at[:, : top.shape[1]], top, sems.at[0]),
+        pltpu.make_async_copy(video.at[:, video.shape[1] - bottom.shape[1] :], bottom, sems.at[1]),
+    ]
+    for load in loads:
+        load.start()
+    for load in loads:
+        load.wait()
 
 
 def masked(values, valid):
@@ -126,6 +132,39 @@
             video, (v0, v1, v2, v3, v4, v5), (weight1_hbm, weight2_hbm),
             table, (weight1, weight2), part1, second, first, slots, sems,
         )
+
+
+def conv_same(maps_ref, weight_ref, taps, rows):
+    total = None
+    for step_t, frame in taps:
+        for step_w in range(3):
+            top, mid, low = (weight_ref[step_t, i, step_w] for i in range(3))
+            rhs = jnp.concatenate([jnp.concatenate([mid, top], 1), jnp.concatenate([low, mid], 1)], 0)
+            left = jnp.concatenate([maps_ref[step_w, frame, r + 1] for r in rows], 0)
+            right = jnp.concatenate([maps_ref[step_w, frame, r + 2] for r in rows], 0)
+            part = jnp.dot(jnp.concatenate([left, right], 1), rhs, preferred_element_type=jnp.float32)
+            total = part if total is None else total + part
+    return total
+
+
+def conv_next(maps_ref, weight_ref, pairs, rows, step_h):
+    total = None
+    for frames, steps in pairs:
+        for step_w in range(3):
+            none = jnp.zeros(weight_ref.shape[3:], weight_ref.dtype)
+            blocks = [[none if t is None else weight_ref[t, step_h, step_w] for t in line] for line in steps]
+            rhs = jnp.concatenate([jnp.concatenate(line, 1) for line in blocks], 0)
+            sides = [jnp.concatenate([maps_ref[step_w, f, r + 3 * (step_h // 2)] for r in rows], 0) for f in frames]
+            part = jnp.dot(jnp.concatenate(sides, 1), rhs, preferred_element_type=jnp.float32)
+            total = part if total is None else total + part
+    return total
+
+
+def gather(same, sides, which, row, width, channels):
+    pair, half = divmod(row, 2)
+    lines = slice(pair * width, (pair + 1) * width)
+    values = same[lines, half * channels : (half + 1) * channels]
+    return values + sides[half][lines, which * channels : (which + 1) * channels]
 
 
 def edge_kernel(
@@ -180,32 +219,6 @@
                 put_shifted(second, to - 2, row, slots, to - 2, values)
 
 
-def conv_same(maps_ref, weight_ref, taps, rows):
-    total = None
-    for step_t, frame in taps:
-        for step_w in range(3):
-            top, mid, low = (weight_ref[step_t, i, step_w] for i in range(3))
-            rhs = jnp.concatenate([jnp.concatenate([mid, top], 1), jnp.concatenate([low, mid], 1)], 0)
-            left = jnp.concatenate([maps_ref[step_w, frame, r + 1] for r in rows], 0)
-            right = jnp.concatenate([maps_ref[step_w, frame, r + 2] for r in rows], 0)
-            part = jnp.dot(jnp.concatenate([left, right], 1), rhs, preferred_element_type=jnp.float32)
-            total = part if total is None else total + part
-    return total
-
-
-def conv_next(maps_ref, weight_ref, pairs, rows, step_h):
-    total = None
-    for frames, steps in pairs:
-        for step_w in range(3):
-            none = jnp.zeros(weight_ref.shape[3:], weight_ref.dtype)
-            blocks = [[none if t is None else weight_ref[t, step_h, step_w] for t in line] for line in steps]
-            rhs = jnp.concatenate([jnp.concatenate(line, 1) for line in blocks], 0)
-            sides = [jnp.concatenate([maps_ref[step_w, f, r + 3 * (step_h // 2)] for r in rows], 0) for f in frames]
-            part = jnp.dot(jnp.concatenate(sides, 1), rhs, preferred_element_type=jnp.float32)
-            total = part if total is None else total + part
-    return total
-
-
 def far_kernel(
     place, video, above, below, behind, behind_above, behind_below, part1, own,
     table, weight1, weight2, out, first, second, slots, held, sems,
@@ -214,74 +227,74 @@
     is_start, has_above, has_below = place()
     g1, s1, b1, g2, s2, b2 = (table[i] for i in range(6))
     g1, s1, g2, s2 = 0.5 * g1, 0.5 * s1, 0.5 * g2, 0.5 * s2
-    clear_slots(slots, width)
-
-    def enter(frame):
+    ins, outs = range(0, rows + 2, 2), range(0, rows, 2)
+    early, late, last = ((0, None), (1, 0)), ((2, 1), (None, 2)), ((0, None), (1, 0))
+
+    def enter(to, sources, frame):
         for row in range(-2, rows + 2):
             at = row + 2 if row < 0 else row - rows if row >= rows else row
-            ref, mine = (behind_above, above) if row < 0 else (behind_below, below) if row >= rows else (behind, video)
-            values = ref[frame, at]
-            if frame >= frames - 2:
-                values = jnp.where(is_start, mine[0, at], values)
-            values = activate(values.astype(jnp.float32), g1, s1)
+            ref = sources[0 if row < 0 else 2 if row >= rows else 1]
+            values = activate(ref[frame, at].astype(jnp.float32), g1, s1)
             values = masked(values, has_above if row < 0 else has_below if row >= rows else None)
-            put_shifted(first, frame, row + 2, slots, frame % 2, values)
-
-    def gather(same, sides, which, row):
-        pair, half = divmod(row, 2)
-        lines = slice(pair * width, (pair + 1) * width)
-        values = same[lines, half * channels : (half + 1) * channels]
-        return values + sides[half][lines, which * channels : (which + 1) * channels]
+            put_shifted(first, to, row + 2, slots, to % 2, values)
 
     def middle(to, same, sides, which, more, group):
         for row in range(rows + 2):
-            values = gather(same, sides, which, row)
+            values = gather(same, sides, which, row, width, channels)
             if more is not None:
                 values = values + pick(more, row, width, channels)
             values = activate(values + b1, g2, s2)
             values = masked(values, has_above if row == 0 else has_below if row == rows + 1 else None)
-            if to < 2:
-                start = row * (width + PAD) + PAD
-                values = jnp.where(is_start, slots[3, start : start + width], values)
             put_shifted(second, to, row, slots, group, values)
 
-    def leave(frame, same, sides, which, more):
+    def leave(frame, same, sides, which, more=None, own_sides=None):
         for row in range(rows):
-            values = gather(same, sides, which, row) + b2
+            values = gather(same, sides, which, row, width, channels) + b2
             if more is not None:
-                values = values + gather(more, own_sides, which, row)
+                values = values + gather(more, own_sides, which, row, width, channels)
             held[frame, row] = (video[frame, row].astype(jnp.float32) + values).astype(out.dtype)
         pltpu.make_async_copy(held.at[frame], out.at[frame], sems.at[frame]).start()
 
-    ins, outs = range(0, rows + 2, 2), range(0, rows, 2)
-    early, late = (((0, 1), ((0, None), (1, 0))), ((2, 3), ((2, 1), (None, 2))))
-    last = ((2, 3), ((0, None), (1, 0)))
-    own3 = conv_same(own, weight2, [(1, 0), (2, 1)], outs)
-    own2 = conv_same(own, weight2, [(2, 0)], outs)
-    own_sides = [conv_next(own, weight2, [((0, 1), ((2, 1), (None, 2)))], outs, h) for h in (0, 2)]
-    enter(3)
-    same = conv_same(first, weight1, [(0, 3)], ins)
-    enter(2)
-    sides = [conv_next(first, weight1, [last], ins, h) for h in (0, 2)]
-    middle(3, same, sides, 1, part1[1], 2)
-    same = conv_same(first, weight1, [(0, 2), (1, 3)], ins)
-    enter(1)
-    middle(2, same, sides, 0, part1[0], 3)
-    enter(0)
-    sides = [conv_next(first, weight1, [late, early], ins, h) for h in (0, 2)]
-    same = conv_same(first, weight1, [(0, 1), (1, 2), (2, 3)], ins)
-    middle(1, same, sides, 1, None, 2)
-    same = conv_same(first, weight1, [(0, 0), (1, 1), (2, 2)], ins)
-    middle(0, same, sides, 0, None, 0)
-    sides = [conv_next(second, weight2, [last], outs, h) for h in (0, 2)]
-    leave(3, conv_same(second, weight2, [(0, 3)], outs), sides, 1, own3)
-    leave(2, conv_same(second, weight2, [(0, 2), (1, 3)], outs), sides, 0, own2)
-    same = conv_same(second, weight2, [(0, 1), (1, 2), (2, 3)], outs)
-    sides = [conv_next(second, weight2, [late, early], outs, h) for h in (0, 2)]
-    leave(1, same, sides, 1, None)
-    leave(0, conv_same(second, weight2, [(0, 0), (1, 1), (2, 2)], outs), sides, 0, None)
-    for frame in range(frames):
-        pltpu.make_async_copy(held.at[frame], out.at[frame], sems.at[frame]).wait()
+    def run(start):
+        clear_slots(slots, width)
+        a, b, c, d = (3, 3, 3, 3) if start else (0, 1, 2, 3)
+        old = (behind_above, behind, behind_below)
+        own3 = conv_same(own, weight2, [(1, 0), (2, 1)], outs)
+        own2 = conv_same(own, weight2, [(2, 0)], outs)
+        own_sides = [conv_next(own, weight2, [((0, 1), late)], outs, h) for h in (0, 2)]
+        if start:
+            enter(d, (above, video, below), 0)
+        else:
+            enter(d, old, d)
+        same = conv_same(first, weight1, [(0, d)], ins)
+        if not start:
+            enter(c, old, c)
+        sides = [conv_next(first, weight1, [((c, d), last)], ins, h) for h in (0, 2)]
+        middle(3, same, sides, 1, part1[1], 2)
+        same = conv_same(first, weight1, [(0, c), (1, d)], ins)
+        if not start:
+            enter(b, old, b)
+        middle(2, same, sides, 0, part1[0], 3)
+        if not start:
+            enter(a, old, a)
+            sides = [conv_next(first, weight1, [((c, d), late), ((a, b), early)], ins, h) for h in (0, 2)]
+            same = conv_same(first, weight1, [(0, b), (1, c), (2, d)], ins)
+            middle(1, same, sides, 1, None, 2)
+            same = conv_same(first, weight1, [(0, a), (1, b), (2, c)], ins)
+            middle(0, same, sides, 0, None, 0)
+        a, b, c, d = (2, 2, 2, 3) if start else (0, 1, 2, 3)
+        sides = [conv_next(second, weight2, [((c, d), last)], outs, h) for h in (0, 2)]
+        leave(3, conv_same(second, weight2, [(0, d)], outs), sides, 1, own3, own_sides)
+        leave(2, conv_same(second, weight2, [(0, c), (1, d)], outs), sides, 0, own2, own_sides)
+        same = conv_same(second, weight2, [(0, b), (1, c), (2, d)], outs)
+        sides = [conv_next(second, weight2, [((c, d), late), ((a, b), early)], outs, h) for h in (0, 2)]
+        leave(1, same, sides, 1)
+        leave(0, conv_same(second, weight2, [(0, a), (1, b), (2, c)], outs), sides, 0)
+        for frame in range(frames):
+            pltpu.make_async_copy(held.at[frame], out.at[frame], sems.at[frame]).wait()
+
+    pl.when(is_start)(functools.partial(run, True))
+    pl.when(jnp.logical_not(is_start))(functools.partial(run, False))
 
 
 VMEM = pl.BlockSpec(memory_space=pltpu.VMEM)
@@ -303,11 +316,12 @@
     return pl.pallas_call(
         ready_kernel,
         out_shape=[edge, edge],
-        in_specs=[VMEM],
+        in_specs=[OUTSIDE],
         out_specs=[VMEM] * 2,
+        scratch_shapes=[pltpu.SemaphoreType.DMA((2,))],
         compiler_params=pltpu.CompilerParams(vmem_limit_bytes=4 * MIB),
         name="ready",
-    )(clip)
+    )(hbm(clip))
 
 
 def near(place, clip, vectors, weight1, weight2):
@@ -411,8 +425,9 @@
     made = near(place, clip, vectors, conv1_weight, conv2_weight)
     below = lax.ppermute(top, "ha", [(h, g) for g, h in up])
     behind_above = lax.ppermute(bottom, ("ha", "ta"), [(at(g, t), at(h, n)) for g, h in up for t, n in on])
-    made = edge(place, clip, above, below, vectors, conv1_weight, conv2_weight, made)
-    part1, own, table, weight1, weight2 = made
+    part1, own, table, weight1, weight2 = edge(
+        place, clip, above, below, vectors, conv1_weight, conv2_weight, made
+    )
     out = far(
         place, clip, above, below, behind, behind_above, behind_below, part1, own, table, weight1, weight2
     )

time: 59.9 us -> 58.6 us (0.978)
  Pallas kernels: 12.8 us -> 9.8 us
  waiting for transfers between devices: 27.4 us -> 29.1 us
    pallas_call x1, Pallas kernels: 5.19 us -> 4.17 us  [far(): pl.pallas_call(functools.partial(far_kernel, place), out_shape=jax.ShapeD...]
    pallas_call x1, Pallas kernels: 5.52 us -> 4.53 us  [edge(): pl.pallas_call(functools.partial(edge_kernel, place), out_shape=[jax.Shap...]
    ppermute x1, waiting for transfers between devices: 22.7 us -> 23.7 us  [body(): lax.ppermute(top, ('ha', 'ta'), [(at(h, t), at(g, n)) for g, h in up for...]
    pallas_call x1, Pallas kernels: 1.08 us -> 0.09 us  [near(): pl.pallas_call(functools.partial(near_kernel, place), out_shape=[jax.Shap...]
    ppermute x1, waiting for transfers between devices: 1.75 us -> 2.73 us  [body(): below = lax.ppermute(top, 'ha', [(h, g) for g, h in up])]
  transfers between devices with their start and end apart: 5 -> 5, of which waited for: 3 -> 3; matrix products, arithmetic and copies ran while one was open for 0% -> 0% of each run, Pallas kernels for 11% -> 8%
where the time goes in v6:
time: 58.6 us; the launch traced here: 58.3 us
  waiting for transfers between devices  29.1 us (50%)
  starting transfers between devices  19.3 us (33%)
  Pallas kernels  9.8 us (17%)
    ppermute x1, waiting for transfers between devices, body(): lax.ppermute(top, ('ha', 'ta'), [(at(h, t), at(g, n)) for g, h in up for...  23.7 us
    ppermute x1, starting transfers between devices, body(): lax.ppermute(bottom, ('ha', 'ta'), [(at(g, t), at(h, n)) for g, h in up f...  7.09 us
    ppermute x1, starting transfers between devices, body(): above = lax.ppermute(bottom, 'ha', up)  6.03 us
    pallas_call x1, Pallas kernels, edge(): pl.pallas_call(functools.partial(edge_kernel, place), out_shape=[jax.Shap...  4.53 us
    pallas_call x1, Pallas kernels, far(): pl.pallas_call(functools.partial(far_kernel, place), out_shape=jax.ShapeD...  4.17 us
    ppermute x1, starting transfers between devices, body(): behind = lax.ppermute(clip, 'ta', on)  3.57 us
    ppermute x1, waiting for transfers between devices, body(): below = lax.ppermute(top, 'ha', [(h, g) for g, h in up])  2.73 us
    ppermute x1, waiting for transfers between devices, body(): behind = lax.ppermute(clip, 'ta', on)  2.7 us
  transfers between devices with their start and end apart: 5, of which 3 were waited for; matrix products, arithmetic and copies ran while one was open for 0% of the time, Pallas kernels for 8%

profile of v6, /device:TPU:66, one launch (start us, length us, event | category | flops | bytes accessed | tf_op | source)
XLA Modules:
  0.0 58.3 jit_solution(7070210245446609535)
XLA Ops:
  0.0 0.0 copy-start
  0.0 1.0 %ready.1 = (bf16[4,2,48,128]{3,2,1,0:T(8,128)(2,1)S(1)}, bf16[4,2,48,128]{3,2,1,0:T(8,128)(2,1)S(1)}) custom-call(bf16[4,8,48,128]{3,2,1,0:T(8,128)(2,1)} %bitcast.8), custom_call_target="tpu_custom_call" | custom-call | tf_op jit(solution)/shard_map/ready/pallas_call | solution.py:316
  1.0 6.0 %collective-permute-start = (bf16[4,2,48,128]{3,2,1,0:T(8,128)(2,1)S(1)}, bf16[4,2,48,128]{3,2,1,0:T(8,128)(2,1)S(1)}, u32[]{:S(2)}, u32[]{:S(2)}) collective-permute-start(bf16[4,2,48,128]{3,2,1,0:T(8,128)(2,1)S(1)} %get-tuple-element.17), channel_id=1, source_target_pairs={{0,16},{16,32},{32,48},{48,64},{64,80},{80,96},{96,112},{112,128},... | collective-permute-start | bytes 294920 | tf_op jit(solution)/shard_map/ppermute | solution.py:424
  7.1 7.1 %collective-permute-start.3 = (bf16[4,2,48,128]{3,2,1,0:T(8,128)(2,1)S(1)}, bf16[4,2,48,128]{3,2,1,0:T(8,128)(2,1)S(1)}, u32[]{:S(2)}, u32[]{:S(2)}) collective-permute-start(bf16[4,2,48,128]{3,2,1,0:T(8,128)(2,1)S(1)} %get-tuple-element.17), channel_id=1, source_target_pairs={{0,18},{2,20},{4,22},{6,24},{8,26},{10,28},{12,30},{16,34},{18,36}... | collective-permute-start | bytes 294920 | tf_op jit(solution)/shard_map/ppermute | solution.py:427
  14.2 1.3 %collective-permute-start.1 = (bf16[4,2,48,128]{3,2,1,0:T(8,128)(2,1)S(1)}, bf16[4,2,48,128]{3,2,1,0:T(8,128)(2,1)S(1)}, u32[]{:S(2)}, u32[]{:S(2)}) collective-permute-start(bf16[4,2,48,128]{3,2,1,0:T(8,128)(2,1)S(1)} %get-tuple-element.18), channel_id=1, source_target_pairs={{16,0},{32,16},{48,32},{64,48},{80,64},{96,80},{112,96},{128,112},... | collective-permute-start | bytes 294920 | tf_op jit(solution)/shard_map/ppermute | solution.py:426
  15.5 1.3 %collective-permute-start.4 = (bf16[4,2,48,128]{3,2,1,0:T(8,128)(2,1)S(1)}, bf16[4,2,48,128]{3,2,1,0:T(8,128)(2,1)S(1)}, u32[]{:S(2)}, u32[]{:S(2)}) collective-permute-start(bf16[4,2,48,128]{3,2,1,0:T(8,128)(2,1)S(1)} %get-tuple-element.18), channel_id=1, source_target_pairs={{16,2},{18,4},{20,6},{22,8},{24,10},{26,12},{28,14},{32,18},{34,20... | collective-permute-start | bytes 294920 | tf_op jit(solution)/shard_map/ppermute | solution.py:423
  16.8 0.0 copy-done
  16.8 3.6 %collective-permute-start.2 = (bf16[4,8,48,128]{3,2,1,0:T(8,128)(2,1)S(1)}, bf16[4,8,48,128]{3,2,1,0:T(8,128)(2,1)S(1)}, u32[]{:S(2)}, u32[]{:S(2)}) collective-permute-start(bf16[4,8,48,128]{3,2,1,0:T(8,128)(2,1)S(1)} %bitcast.9), channel_id=1, source_target_pairs={{0,2},{2,4},{4,6},{6,8},{8,10},{10,12},{12,14},{1,3},{3,5},{5,7},{... | collective-permute-start | bytes 1179656 | tf_op jit(solution)/shard_map/ppermute | solution.py:421
  20.4 0.1 near.1
  20.5 0.0 collective-permute-done.above
  20.5 2.7 %collective-permute-done.1.below = bf16[4,2,48,128]{3,2,1,0:T(8,128)(2,1)S(1)} collective-permute-done((bf16[4,2,48,128]{3,2,1,0:T(8,128)(2,1)S(1)}, bf16[4,2,48,128]{3,2,1,0:T(8,128)(2,1)S(1)}, u32[]{:S(2)}, u32[]{:S(2)}) %collective-permute-start.1) | collective-permute-done | bytes 98336 | tf_op jit(solution)/shard_map/ppermute | solution.py:426
  23.2 4.5 %edge.1 = (f32[4,240,256]{2,1,0:T(8,128)S(1)}, bf16[3,2,10,48,128]{4,3,2,1,0:T(8,128)(2,1)S(1)}, f32[6,1,128]{2,1,0:T(1,128)S(1)}, bf16[3,3,3,128,128]{4,3,2,1,0...) custom-call(bf16[4,8,48,128]{3,2,1,0:T(8,128)(2,1)S(1)} %bitcast.11,, ...), custom_call_target="tpu_custom_call", output_to_operand_aliasing={{0}: (11, {}), {1}: (12, {}), {2}: (13, {}), {3}: (14, {}),... | custom-call | flops 2000000000 | bytes 4000000 | tf_op jit(solution)/shard_map/edge/pallas_call | solution.py:357
  27.7 0.0 collective-permute-done.3.behind_above
  27.8 23.7 %collective-permute-done.4.behind_below = bf16[4,2,48,128]{3,2,1,0:T(8,128)(2,1)S(1)} collective-permute-done((bf16[4,2,48,128]{3,2,1,0:T(8,128)(2,1)S(1)}, bf16[4,2,48,128]{3,2,1,0:T(8,128)(2,1)S(1)}, u32[]{:S(2)}, u32[]{:S(2)}) %collective-permute-start.4) | collective-permute-done | bytes 98336 | tf_op jit(solution)/shard_map/ppermute | solution.py:423
  51.5 2.7 %collective-permute-done.2.behind = bf16[4,8,48,128]{3,2,1,0:T(8,128)(2,1)S(1)} collective-permute-done((bf16[4,8,48,128]{3,2,1,0:T(8,128)(2,1)S(1)}, bf16[4,8,48,128]{3,2,1,0:T(8,128)(2,1)S(1)}, u32[]{:S(2)}, u32[]{:S(2)}) %collective-permute-start.2) | collective-permute-done | bytes 393248 | tf_op jit(solution)/shard_map/ppermute | solution.py:421
  54.2 4.2 %far.1 = bf16[4,8,48,128]{3,2,1,0:T(8,128)(2,1)} custom-call(bf16[4,8,48,128]{3,2,1,0:T(8,128)(2,1)S(1)} %bitcast.12, bf16[4,2,48,128]{3,2,1,0:T(8,128)(2,1)S(1)} %collective-permute-done.above, bf16[4,2,48,128]{3,2,1,0:T(8,128)(2,1)S(1)} %collective-permute-done.1.below, bf16[4,8,48,128]{3,2,1,0:T(8,128)(2,1)S(1)} %collective-permute-done.2.behind, ...), custom_call_target="tpu_custom_call" | custom-call | flops 4000000000 | bytes 4000000 | tf_op jit(solution)/shard_map/far/pallas_call | solution.py:378
Async XLA Ops:
  0.0 16.8 %copy-start = (bf16[1,4,8,48,128]{4,3,2,1,0:T(8,128)(2,1)S(1)}, bf16[1,4,8,48,128]{4,3,2,1,0:T(8,128)(2,1)}, u32[]{:S(2)}) copy-start(bf16[1,4,8,48,128]{4,3,2,1,0:T(8,128)(2,1)} %param.9) | copy-start | bytes 1179652
  1.0 19.5 %collective-permute-start = (bf16[4,2,48,128]{3,2,1,0:T(8,128)(2,1)S(1)}, bf16[4,2,48,128]{3,2,1,0:T(8,128)(2,1)S(1)}, u32[]{:S(2)}, u32[]{:S(2)}) collective-permute-start(bf16[4,2,48,128]{3,2,1,0:T(8,128)(2,1)S(1)} %get-tuple-element.17), channel_id=1, source_target_pairs={{0,16},{16,32},{32,48},{48,64},{64,80},{80,96},{96,112},{112,128},... | collective-permute-start | bytes 294920 | tf_op jit(solution)/shard_map/ppermute | solution.py:424
  7.1 20.7 %collective-permute-start.3 = (bf16[4,2,48,128]{3,2,1,0:T(8,128)(2,1)S(1)}, bf16[4,2,48,128]{3,2,1,0:T(8,128)(2,1)S(1)}, u32[]{:S(2)}, u32[]{:S(2)}) collective-permute-start(bf16[4,2,48,128]{3,2,1,0:T(8,128)(2,1)S(1)} %get-tuple-element.17), channel_id=1, source_target_pairs={{0,18},{2,20},{4,22},{6,24},{8,26},{10,28},{12,30},{16,34},{18,36}... | collective-permute-start | bytes 294920 | tf_op jit(solution)/shard_map/ppermute | solution.py:427
  14.2 9.1 %collective-permute-start.1 = (bf16[4,2,48,128]{3,2,1,0:T(8,128)(2,1)S(1)}, bf16[4,2,48,128]{3,2,1,0:T(8,128)(2,1)S(1)}, u32[]{:S(2)}, u32[]{:S(2)}) collective-permute-start(bf16[4,2,48,128]{3,2,1,0:T(8,128)(2,1)S(1)} %get-tuple-element.18), channel_id=1, source_target_pairs={{16,0},{32,16},{48,32},{64,48},{80,64},{96,80},{112,96},{128,112},... | collective-permute-start | bytes 294920 | tf_op jit(solution)/shard_map/ppermute | solution.py:426
  15.5 36.0 %collective-permute-start.4 = (bf16[4,2,48,128]{3,2,1,0:T(8,128)(2,1)S(1)}, bf16[4,2,48,128]{3,2,1,0:T(8,128)(2,1)S(1)}, u32[]{:S(2)}, u32[]{:S(2)}) collective-permute-start(bf16[4,2,48,128]{3,2,1,0:T(8,128)(2,1)S(1)} %get-tuple-element.18), channel_id=1, source_target_pairs={{16,2},{18,4},{20,6},{22,8},{24,10},{26,12},{28,14},{32,18},{34,20... | collective-permute-start | bytes 294920 | tf_op jit(solution)/shard_map/ppermute | solution.py:423
  16.8 37.4 %collective-permute-start.2 = (bf16[4,8,48,128]{3,2,1,0:T(8,128)(2,1)S(1)}, bf16[4,8,48,128]{3,2,1,0:T(8,128)(2,1)S(1)}, u32[]{:S(2)}, u32[]{:S(2)}) collective-permute-start(bf16[4,8,48,128]{3,2,1,0:T(8,128)(2,1)S(1)} %bitcast.9), channel_id=1, source_target_pairs={{0,2},{2,4},{4,6},{6,8},{8,10},{10,12},{12,14},{1,3},{3,5},{5,7},{... | collective-permute-start | bytes 1179656 | tf_op jit(solution)/shard_map/ppermute | solution.py:421
